TPU v7x, 32 devices: a whole 2x2x4 slice. The times are simulated.
32 devices in a mesh: shard: 8 (over z, x), width: 4 (over y, core).
Axes of the slice: x: 2, y: 2, z: 4, core: 2. Of those that a mesh axis runs over, the one named last changes fastest.
Arguments:
- w_gate: bfloat16 [2048, 8192], P('shard', 'width'), may hold values from -0.125 to 0.125
- low_gate: bfloat16 [2048, 64], P('shard'), may hold values from -0.125 to 0.125
- high_gate: bfloat16 [64, 8192], P(None, 'width'), may hold values from -0.75 to 0.75
- w_up: bfloat16 [2048, 8192], P('shard', 'width'), may hold values from -0.125 to 0.125
- low_up: bfloat16 [2048, 64], P('shard'), may hold values from -0.125 to 0.125
- high_up: bfloat16 [64, 8192], P(None, 'width'), may hold values from -0.75 to 0.75
- w_down: bfloat16 [8192, 2048], P('width', 'shard'), may hold values from -0.0625 to 0.0625
- low_down: bfloat16 [8192, 64], P('width'), may hold values from -0.0625 to 0.0625
- high_down: bfloat16 [64, 2048], P(None, 'shard'), may hold values from -0.75 to 0.75
- norm_train: float32 [2048], P(('shard', 'width')), may hold values from 0.25 to 1.75
- norm_step: float32 [2048], P(('shard', 'width')), may hold values from -0.3 to 0.3
Outputs:
- serve_gate: bfloat16 [8192, 2048], P('width')
- serve_up: bfloat16 [8192, 2048], P('width')
- serve_down: bfloat16 [2048, 8192], P(None, 'width')
- serve_norm: bfloat16 [2048], replicated
All inputs are finite; a program needn't handle non-finite values.
Results may differ from a plain program's by a relative error of at most 0.001.
Values may be sent and summed in bfloat16 or wider, within the bound.
A program may use at most 128 MiB of HBM per device.

v0:
```python
import functools

import jax
import jax.numpy as jnp
from jax import lax
from jax.experimental import pallas as pl
from jax.experimental.pallas import tpu as pltpu
from jax.sharding import PartitionSpec as P

mix_rate = 2.0
MESH = pl.DeviceIdType.MESH
X = 2


def merged(w, low, high):
    fresh = w.astype(jnp.float32) + mix_rate * jnp.dot(
        low, high, preferred_element_type=jnp.float32
    )
    return fresh.astype(jnp.bfloat16)


PIECES = ((0, 0), (1, 0), (2, 0), (0, 1), (1, 1), (2, 1))
LINE = tuple(range(len(PIECES) - 1))
PAIR = len(PIECES) - 1
UP, DOWN, SIDE = 0, 1, 2
STRIP = 128


def gather_kernel(
    shards, widths, gate, up, down, norm, o_gate, o_up, o_down, o_norm,
    send_sem, recv_sem, norm_send, norm_recv, own_sem,
):
    lines = shards // X
    me, w = lax.axis_index("shard"), lax.axis_index("width")
    z, x = me // X, me % X
    partner = z * X + (1 - x)
    blocks, outs = (gate, up, down), (o_gate, o_up, o_down)
    n_pieces = len(PIECES)

    def own(c):
        t, h = PIECES[c]
        ref = blocks[t]
        if t < 2:
            half = ref.shape[0] // 2
            return ref.at[pl.ds(h * half, half), :]
        half = ref.shape[1] // 2
        return ref.at[:, pl.ds(h * half, half)]

    def place(s, c):
        t, h = PIECES[c]
        ref, out = blocks[t], outs[t]
        if t < 2:
            half, wide = ref.shape[0] // 2, ref.shape[1]
            return out.at[pl.ds(h * half, half), pl.ds(pl.multiple_of(s * wide, wide), wide)]
        half, tall = ref.shape[1] // 2, ref.shape[0]
        return out.at[pl.ds(pl.multiple_of(s * tall, tall), tall), pl.ds(h * half, half)]

    def target(way):
        return {UP: me + X, DOWN: me - X, SIDE: partner}[way]

    sends = []

    def when(conds, fn):
        if conds is None:
            fn()
        else:
            pl.when(conds)(fn)

    def has(way):
        return {UP: z + 1 < lines, DOWN: z > 0, SIDE: None}[way]

    def both(a, b):
        if a is None:
            return b
        if b is None:
            return a
        return jnp.logical_and(a, b)

    def send(way, s, c, slot, cond, from_own=False):
        def make():
            return pltpu.make_async_remote_copy(
                src_ref=own(c) if from_own else place(s, c),
                dst_ref=place(s, c),
                send_sem=send_sem.at[way, slot],
                recv_sem=recv_sem.at[s * n_pieces + c],
                device_id=(target(way), w),
                device_id_type=MESH,
            )

        full = both(cond, has(way))
        when(full, lambda: make().start())
        sends.append((full, lambda: make().wait_send()))

    def arrive(s, c, cond=None):
        when(
            cond,
            lambda: pltpu.make_async_remote_copy(
                src_ref=place(s, c),
                dst_ref=place(s, c),
                send_sem=send_sem.at[0, 0],
                recv_sem=recv_sem.at[s * n_pieces + c],
                device_id=(partner, w),
                device_id_type=MESH,
            ).wait_recv(),
        )

    def norm_rows(first, count):
        return o_norm.at[pl.ds(first, count)]

    def norm_copy(src, first, count, sem, rsem, dev):
        return pltpu.make_async_remote_copy(
            src_ref=src, dst_ref=norm_rows(first, count), send_sem=norm_send.at[sem],
            recv_sem=norm_recv.at[rsem], device_id=dev, device_id_type=MESH,
        )

    barrier = pltpu.get_barrier_semaphore()
    peers = [lax.rem(w + k, widths) for k in range(1, widths)]
    for p in peers:
        pl.semaphore_signal(barrier, inc=1, device_id=(me, p), device_id_type=MESH)
    for way in (UP, DOWN, SIDE):
        when(
            has(way),
            lambda way=way: pl.semaphore_signal(
                barrier, inc=1, device_id=(target(way), w), device_id_type=MESH
            ),
        )
    inner = jnp.logical_and(z > 0, z + 1 < lines)
    pl.when(inner)(lambda: pl.semaphore_wait(barrier, widths + 2))
    ends = widths + (1 if lines > 1 else 0)
    pl.when(jnp.logical_not(inner))(lambda: pl.semaphore_wait(barrier, ends))

    send(SIDE, me, PAIR, PAIR, None, from_own=True)
    for c in LINE:
        send(UP, me, c, c, None, from_own=True)
        send(DOWN, me, c, c, None, from_own=True)
        send(SIDE, me, c, c, None, from_own=True)
    norm_own = pltpu.make_async_copy(norm, norm_rows(me * widths + w, 1), own_sem.at[0])
    norm_own.start()
    tile_of = lambda k: norm_copy(norm, me * widths + w, 1, k - 1, k - 1, (me, peers[k - 1]))
    for k in range(1, widths):
        tile_of(k).start()
    norm_own.wait()
    for k in range(1, widths):
        source = lax.rem(w + widths - k, widths)
        norm_copy(norm, me * widths + source, 1, k - 1, k - 1, (me, peers[k - 1])).wait_recv()
    side_at = widths - 1
    norm_side = lambda s: norm_copy(
        norm_rows(s * widths, widths), s * widths, widths, side_at, side_at, (partner, w)
    )
    norm_side(me).start()

    wide, tall = gate.shape[1], down.shape[0]
    columns = pl.ds(pl.multiple_of(me * wide, wide), wide)

    @pl.loop(0, gate.shape[0] // STRIP)
    def _(i):
        rows = pl.ds(pl.multiple_of(i * STRIP, STRIP), STRIP)
        o_gate[rows, columns] = gate[rows, :]
        o_up[rows, columns] = up[rows, :]

    @pl.loop(0, tall // 16)
    def _(i):
        rows = pl.ds(pl.multiple_of(i * 16, 16), 16)
        o_down[pl.ds(pl.multiple_of(me * tall + i * 16, 16), 16), :] = down[rows, :]

    for d in range(1, lines):
        for c in LINE:
            for way, s, cond in (
                (UP, me - d * X, z >= d),
                (DOWN, me + d * X, z + d < lines),
            ):
                arrive(s, c, cond)
                slot = d * n_pieces + c
                send(way, s, c, slot, cond)
                send(SIDE, s, c, slot + (way * lines * n_pieces), cond)

    arrive(partner, PAIR)
    norm_side(partner).wait_recv()

    def norm_pair(way, plane):
        rows = X * widths
        at = widths + way * lines
        return norm_copy(
            norm_rows(plane * rows, rows), plane * rows, rows,
            at + (plane - z) * (1 - 2 * way) * -1, widths + plane, (target(way), w),
        )

    line_slot = 2 * lines * n_pieces
    for d in range(lines):
        for way, plane, cond in (
            (UP, z - d, z >= d),
            (DOWN, z + d, z + d < lines),
        ):
            if d == 0:
                cond = None
            for j in range(X):
                s = me if (d == 0 and j == 0) else (partner if d == 0 else plane * X + j)
                if d > 0:
                    arrive(s, PAIR, cond)
                send(way, s, PAIR, line_slot + d * X + j, cond, from_own=(d == 0 and j == 0))
            full = both(cond, has(way))
            if d > 0:
                when(cond, lambda way=way, plane=plane: norm_pair(way, plane).wait_recv())
            when(full, lambda way=way, plane=plane: norm_pair(way, plane).start())
            sends.append((full, lambda way=way, plane=plane: norm_pair(way, plane).wait_send()))

    for c in LINE:
        arrive(partner, c)
    for d in range(1, lines):
        for c in LINE:
            arrive(partner - d * X, c, z >= d)
            arrive(partner + d * X, c, z + d < lines)
    for k in range(1, widths):
        tile_of(k).wait_send()
    norm_side(me).wait_send()
    for cond, wait in sends:
        when(cond, wait)


def gather_all(shards, widths, gate, up, down, norm):
    lines = shards // X
    n_pieces = len(PIECES)
    any_ = pl.BlockSpec(memory_space=pl.ANY)
    vmem = pl.BlockSpec(memory_space=pltpu.VMEM)
    wide = lambda b: pltpu.VMEM((b.shape[0], shards * b.shape[1]), b.dtype)
    tall = lambda b: pltpu.VMEM((shards * b.shape[0], b.shape[1]), b.dtype)
    return pl.pallas_call(
        functools.partial(gather_kernel, shards, widths),
        out_shape=(
            wide(gate), wide(up), tall(down),
            pltpu.HBM((shards * widths,) + norm.shape[1:], norm.dtype),
        ),
        in_specs=[vmem] * 4,
        out_specs=(vmem,) * 3 + (any_,),
        scratch_shapes=[
            pltpu.SemaphoreType.DMA((3, 2 * lines * n_pieces + lines * X)),
            pltpu.SemaphoreType.DMA((shards * n_pieces,)),
            pltpu.SemaphoreType.DMA((widths + 2 * lines,)),
            pltpu.SemaphoreType.DMA((widths + lines,)),
            pltpu.SemaphoreType.DMA((1,)),
        ],
        compiler_params=pltpu.CompilerParams(collective_id=0, has_side_effects=True, vmem_limit_bytes=16 * 2**20),
    )(gate, up, down, norm)


def write_kernel(gate, up, down, tiles, o_gate, o_up, o_down, o_tiles, sem):
    pairs = ((gate, o_gate), (up, o_up), (down, o_down))
    copies = [pltpu.make_async_copy(a, b, sem.at[i]) for i, (a, b) in enumerate(pairs)]
    for copy in copies:
        copy.start()
    o_tiles[...] = tiles[...]
    for copy in copies:
        copy.wait()


def write_out(gate, up, down, tiles):
    any_ = pl.BlockSpec(memory_space=pl.ANY)
    vmem = pl.BlockSpec(memory_space=pltpu.VMEM)
    return pl.pallas_call(
        write_kernel,
        out_shape=tuple(jax.ShapeDtypeStruct(a.shape, a.dtype) for a in (gate, up, down, tiles)),
        in_specs=[any_] * 3 + [vmem],
        out_specs=(any_,) * 3 + (vmem,),
        scratch_shapes=[pltpu.SemaphoreType.DMA((3,))],
        compiler_params=pltpu.CompilerParams(vmem_limit_bytes=4 * 2**20),
    )(gate, up, down, tiles)


def body(
    shards,
    widths,
    w_gate,
    low_gate,
    high_gate,
    w_up,
    low_up,
    high_up,
    w_down,
    low_down,
    high_down,
    norm_train,
    norm_step,
):
    gate = merged(w_gate, low_gate, high_gate)
    up = merged(w_up, low_up, high_up)
    down = merged(w_down, low_down, high_down)
    gain = norm_train + norm_step
    if shards % X or gate.shape[0] % 128 or down.shape[0] % 256 or gate.shape[0] % STRIP or gain.shape[0] > 128:
        gate, up, down = (
            lax.all_gather(gate, "shard", axis=0, tiled=True),
            lax.all_gather(up, "shard", axis=0, tiled=True),
            lax.all_gather(down, "shard", axis=1, tiled=True),
        )
        gain = lax.all_gather(gain.astype(jnp.bfloat16), ("shard", "width"), axis=0, tiled=True)
        return gate.T, up.T, down.T, gain
    count = gain.shape[0]
    tile = jnp.pad(gain.reshape(1, 1, count), ((0, 0), (0, 7), (0, 128 - count)))
    gate, up, down, tiles = gather_all(shards, widths, gate.T, up.T, down.T, tile)
    gate, up, down, tiles = write_out(gate, up, down, tiles)
    return gate, up, down, tiles[:, 0, :count].reshape(-1).astype(jnp.bfloat16)


def solution(mesh):
    return jax.shard_map(
        functools.partial(body, mesh.shape["shard"], mesh.shape["width"]),
        mesh=mesh,
        in_specs=(
            P("shard", "width"),
            P("shard", None),
            P(None, "width"),
            P("shard", "width"),
            P("shard", None),
            P(None, "width"),
            P("width", "shard"),
            P("width", None),
            P(None, "shard"),
            P(("shard", "width")),
            P(("shard", "width")),
        ),
        out_specs=(P("width", None), P("width", None), P(None, "width"), P()),
        check_vma=False,
    )
```

profile of v0, /device:TPU:0, one launch (start us, length us, event | category | flops | bytes accessed | tf_op | source)
XLA Modules:
  0.0 267.1 jit_solution(270420570686985209)
XLA Ops:
  0.6 0.0 copy-start
  0.6 0.0 copy-start.2
  0.7 0.7 add_bitcast_fusion
  1.4 1.5 copy.21
  2.9 0.0 copy-done
  2.9 0.0 copy-done.2
  2.9 0.0 copy-start.3
  2.9 0.5 fusion.8.gate
  3.4 1.5 copy.23
  4.9 0.0 copy-done.3
  4.9 0.0 copy-start.4
  4.9 1.5 fusion.7.up
  6.4 1.5 copy.25
  7.9 0.0 copy-done.4
  7.9 1.4 fusion.6.down
  9.3 247.4 %shard_map.138 = (bf16[2048,2048]{1,0:T(8,128)(2,1)S(1)}, bf16[2048,2048]{1,0:T(8,128)(2,1)S(1)}, bf16[2048,2048]{1,0:T(8,128)(2,1)S(1)}, f32[32,8,128]{2,1,0:T(8,128)}) custom-call(bf16[2048,256]{1,0:T(8,128)(2,1)S(1)} %fusion.8.gate, bf16[2048,256]{1,0:T(8,128)(2,1)S(1)} %fusion.7.up, bf16[256,2048]{1,0:T(8,128)(2,1)S(1)} %fusion.6.down, ...), custom_call_target="tpu_custom_call" | custom-call | tf_op jit(solution)/shard_map/pallas_call | solution.py:227
  256.8 0.0 copy-start.1
  256.8 0.9 copy-done.1
  257.7 8.7 %shard_map.139 = (bf16[2048,2048]{1,0:T(8,128)(2,1)}, bf16[2048,2048]{1,0:T(8,128)(2,1)}, bf16[2048,2048]{1,0:T(8,128)(2,1)}, f32[32,8,128]{2,1,0:T(8,128)S(1)}) custom-call(bf16[2048,2048]{1,0:T(8,128)(2,1)S(1)} %get-tuple-element.12.gate, bf16[2048,2048]{1,0:T(8,128)(2,1)S(1)} %get-tuple-element.13.up, bf16[2048,2048]{1,0:T(8,128)(2,1)S(1)} %get-tuple-element.14.down, ...), custom_call_target="tpu_custom_call" | custom-call | tf_op jit(solution)/shard_map/pallas_call | solution.py:259
  266.4 0.1 fusion.9
  266.4 0.7 convert_element_type.30
  (1 shorter events, 0.0 us)
Async XLA Ops:
  0.6 2.2 copy-start
  0.6 2.2 copy-start.2
  2.9 2.0 copy-start.3
  4.9 3.0 %copy-start.4 = (bf16[64,256]{1,0:T(8,128)(2,1)S(1)}, bf16[64,256]{1,0:T(8,128)(2,1)}, u32[]{:S(2)}) copy-start(bf16[64,256]{1,0:T(8,128)(2,1)} %param.19) | copy-start | bytes 98308
  256.8 0.9 copy-start.1
where the time goes:
time: 267 us
  Pallas kernels  256 us (96%)
  local copies, waits for them, and re-layouts  6.1 us (2%)
  matrix products  3.38 us (1%)
    pallas_call x1, Pallas kernels, gather_all(): pl.pallas_call(functools.partial(gather_kernel, shards, widths), out_shap...  247 us
    pallas_call x1, Pallas kernels, write_out(): pl.pallas_call(write_kernel, out_shape=tuple((jax.ShapeDtypeStruct(a.shap...  8.7 us
    unnamed x13, local copies, waits for them, and re-layouts  5.37 us

commit v1 on v0

v1 whole, which is shorter than its diff:
```python
import functools

import jax
import jax.numpy as jnp
from jax import lax
from jax.experimental import pallas as pl
from jax.experimental.pallas import tpu as pltpu
from jax.sharding import PartitionSpec as P

mix_rate = 2.0
MESH = pl.DeviceIdType.MESH
X = 2
LANES = 128

CUTS = 4
LINE = ((0, 0), (0, 1), (1, 0), (0, 2), (1, 1), (2, 0), (0, 3), (1, 2), (2, 1), (2, 2))
PAIR = ((1, 3), (2, 3))
ORDER = LINE[:2] + PAIR[:1] + LINE[2:6] + PAIR[1:] + LINE[6:]
UP, DOWN, SIDE = 0, 1, 2
WAYS = 3
N_PIECES = 3 * CUTS


def merged(w, low, high):
    fresh = w.astype(jnp.float32) + mix_rate * jnp.dot(
        low, high, preferred_element_type=jnp.float32
    )
    return fresh.astype(jnp.bfloat16)


def when(cond, fn):
    if cond is None:
        fn()
    else:
        pl.when(cond)(fn)


def both(a, b):
    if a is None:
        return b
    if b is None:
        return a
    return jnp.logical_and(a, b)


def gather_kernel(
    shards, widths,
    w_gate, low_gate, high_gate, w_up, low_up, high_up, w_down, low_down, high_down, train, step,
    o_gate, o_up, o_down, o_norm,
    v_gate, v_up, v_down, v_low_gate, v_low_up, v_low_down, v_high_gate, v_high_up, v_high_down,
    v_train, v_step, l_gate, l_up, h_down,
    send_sem, recv_sem, norm_send, norm_recv, load_sem, small_sem,
):
    lines = shards // X
    me, w = lax.axis_index("shard"), lax.axis_index("width")
    z, x = me // X, me % X
    partner = z * X + (1 - x)
    outs = (o_gate, o_up, o_down)
    big = ((w_gate, v_gate), (w_up, v_up), (w_down, v_down))
    wide = w_gate.shape[0]
    cut = w_gate.shape[1] // CUTS

    def load(c):
        t, h = c
        src, dst = big[t]
        at = (slice(None), pl.ds(h * cut, cut)) if t < 2 else (pl.ds(h * cut, cut), slice(None))
        return pltpu.make_async_copy(src.at[at], dst.at[at], load_sem.at[t * CUTS + h])

    smalls = [
        (low_gate, v_low_gate), (high_gate, v_high_gate),
        (low_up, v_low_up), (high_up, v_high_up),
        (low_down, v_low_down), (high_down, v_high_down),
        (train, v_train), (step, v_step),
    ]
    small = [pltpu.make_async_copy(a, b, small_sem.at[i]) for i, (a, b) in enumerate(smalls)]
    first = {0: small[0:2], 1: small[2:4], 2: small[4:6]}
    started = set()
    for c in ORDER:
        if c[0] not in started:
            started.add(c[0])
            for copy in first[c[0]]:
                copy.start()
        load(c).start()
    for copy in small[6:]:
        copy.start()

    def target(way):
        return {UP: me + X, DOWN: me - X, SIDE: partner}[way]

    def has(way):
        return {UP: z + 1 < lines, DOWN: z > 0, SIDE: None}[way]

    barrier = pltpu.get_barrier_semaphore()
    peers = [lax.rem(w + k, widths) for k in range(1, widths)]
    for way in (UP, DOWN, SIDE):
        when(
            has(way),
            lambda way=way: pl.semaphore_signal(
                barrier, inc=1, device_id=(target(way), w), device_id_type=MESH
            ),
        )
    for p in peers:
        pl.semaphore_signal(barrier, inc=1, device_id=(me, p), device_id_type=MESH)

    def place(s, c):
        t, h = c
        at = pl.ds(pl.multiple_of(s * wide, wide), wide)
        return outs[t].at[pl.ds(h * cut, cut), at] if t < 2 else outs[t].at[at, pl.ds(h * cut, cut)]

    slots = {}
    sends = []

    def index(c):
        return c[0] * CUTS + c[1]

    def send(way, s, c, cond):
        slot = slots.get(way, 0)
        slots[way] = slot + 1

        def make():
            return pltpu.make_async_remote_copy(
                src_ref=place(s, c),
                dst_ref=place(s, c),
                send_sem=send_sem.at[way, slot],
                recv_sem=recv_sem.at[s * N_PIECES + index(c)],
                device_id=(target(way), w),
                device_id_type=MESH,
            )

        full = both(cond, has(way))
        when(full, lambda: make().start())
        sends.append((full, lambda: make().wait_send()))

    def arrive(s, c, cond=None):
        when(
            cond,
            lambda: pltpu.make_async_remote_copy(
                src_ref=place(s, c),
                dst_ref=place(s, c),
                send_sem=send_sem.at[0, 0],
                recv_sem=recv_sem.at[s * N_PIECES + index(c)],
                device_id=(partner, w),
                device_id_type=MESH,
            ).wait_recv(),
        )

    seen = set()

    def compute(c):
        t, h = c
        if t not in seen:
            seen.add(t)
            for copy in first[t]:
                copy.wait()
            if t == 0:
                l_gate[...] = v_low_gate[...].T
            elif t == 1:
                l_up[...] = v_low_up[...].T
            else:
                h_down[...] = v_high_down[...].T
        load(c).wait()
        columns = pl.ds(pl.multiple_of(me * wide, wide), wide)

        @pl.loop(0, cut // LANES)
        def _(i):
            at = pl.ds(pl.multiple_of(h * cut + i * LANES, LANES), LANES)
            if t < 2:
                block, low, high = ((v_gate, l_gate, v_high_gate), (v_up, l_up, v_high_up))[t]
                outs[t][at, columns] = merged(block[:, at], low[...], high[:, at]).T
            else:
                o_down[columns, at] = merged(v_down[at, :].T, h_down[...], v_low_down[:, at])

    def send_own(c):
        if c in LINE:
            send(UP, me, c, None)
            send(DOWN, me, c, None)
        send(SIDE, me, c, None)

    compute(ORDER[0])
    inner = jnp.logical_and(z > 0, z + 1 < lines)
    pl.when(inner)(lambda: pl.semaphore_wait(barrier, widths + 2))
    ends = widths + (1 if lines > 1 else 0)
    pl.when(jnp.logical_not(inner))(lambda: pl.semaphore_wait(barrier, ends))
    for k, c in enumerate(ORDER):
        if k:
            compute(c)
        send_own(c)

    def norm_rows(begin, count):
        return o_norm.at[pl.ds(begin, count)]

    def norm_copy(begin, count, sem, rsem, dev):
        return pltpu.make_async_remote_copy(
            src_ref=norm_rows(begin, count), dst_ref=norm_rows(begin, count),
            send_sem=norm_send.at[sem], recv_sem=norm_recv.at[rsem],
            device_id=dev, device_id_type=MESH,
        )

    for copy in small[6:]:
        copy.wait()
    gain = v_train[...] + v_step[...]
    row = jnp.concatenate([gain] * (LANES // gain.shape[1]), axis=1)
    o_norm[pl.ds(me * widths + w, 1)] = row.reshape(1, 1, LANES)
    tile_of = lambda k: norm_copy(me * widths + w, 1, k - 1, k - 1, (me, peers[k - 1]))
    for k in range(1, widths):
        tile_of(k).start()
    side_at = widths - 1
    norm_side = lambda s: norm_copy(s * widths, widths, side_at, side_at, (partner, w))

    def norm_gather():
        for k in range(1, widths):
            source = lax.rem(w + widths - k, widths)
            norm_copy(me * widths + source, 1, k - 1, k - 1, (me, peers[k - 1])).wait_recv()
        norm_side(me).start()

    for d in range(1, lines):
        for c in LINE:
            for way, s, cond in (
                (UP, me - d * X, z >= d),
                (DOWN, me + d * X, z + d < lines),
            ):
                arrive(s, c, cond)
                send(way, s, c, cond)
                send(SIDE, s, c, cond)
        if d == 1:
            norm_gather()
    if lines == 1:
        norm_gather()

    for c in PAIR:
        arrive(partner, c)
    norm_side(partner).wait_recv()

    def norm_pair(way, plane):
        rows = X * widths
        at = widths + way * lines
        return norm_copy(
            plane * rows, rows, at + (plane - z) * (1 - 2 * way) * -1, widths + plane, (target(way), w)
        )

    for d in range(lines):
        for way, plane, cond in (
            (UP, z - d, z >= d),
            (DOWN, z + d, z + d < lines),
        ):
            if d == 0:
                cond = None
            full = both(cond, has(way))
            if d > 0:
                when(cond, lambda way=way, plane=plane: norm_pair(way, plane).wait_recv())
            when(full, lambda way=way, plane=plane: norm_pair(way, plane).start())
            sends.append((full, lambda way=way, plane=plane: norm_pair(way, plane).wait_send()))
            for c in PAIR:
                for j in range(X):
                    s = (me if j == 0 else partner) if d == 0 else plane * X + j
                    if d > 0:
                        arrive(s, c, cond)
                    send(way, s, c, cond)

    for c in LINE:
        arrive(partner, c)
    for d in range(1, lines):
        for c in LINE:
            arrive(partner - d * X, c, z >= d)
            arrive(partner + d * X, c, z + d < lines)
    for k in range(1, widths):
        tile_of(k).wait_send()
    norm_side(me).wait_send()
    for cond, wait in sends:
        when(cond, wait)


def gather_all(shards, widths, args):
    lines = shards // X
    w_gate, low_gate, high_gate, w_up, low_up, high_up, w_down, low_down, high_down, train, step = args
    hbm = pl.BlockSpec(memory_space=pltpu.HBM)
    vmem = pl.BlockSpec(memory_space=pltpu.VMEM)
    like = lambda a: pltpu.VMEM(a.shape, a.dtype)
    flip = lambda a: pltpu.VMEM(a.shape[::-1], a.dtype)
    wide, tall = w_gate.shape
    full = pltpu.VMEM((tall, shards * wide), w_gate.dtype)
    long = len(LINE) * lines + len(PAIR) * lines * X
    return pl.pallas_call(
        functools.partial(gather_kernel, shards, widths),
        out_shape=(
            full, full,
            pltpu.VMEM((shards * wide, tall), w_down.dtype),
            pltpu.VMEM((shards * widths, 1, LANES), train.dtype),
        ),
        in_specs=[hbm] * len(args),
        out_specs=(vmem,) * 4,
        scratch_shapes=[
            like(w_gate), like(w_up), like(w_down),
            like(low_gate), like(low_up), like(low_down),
            like(high_gate), like(high_up), like(high_down),
            like(train), like(step),
            flip(low_gate), flip(low_up), flip(high_down),
            pltpu.SemaphoreType.DMA((WAYS, max(long, N_PIECES + 2 * len(LINE) * lines))),
            pltpu.SemaphoreType.DMA((shards * N_PIECES,)),
            pltpu.SemaphoreType.DMA((widths + 2 * lines,)),
            pltpu.SemaphoreType.DMA((widths + lines,)),
            pltpu.SemaphoreType.DMA((N_PIECES,)),
            pltpu.SemaphoreType.DMA((8,)),
        ],
        compiler_params=pltpu.CompilerParams(collective_id=0, has_side_effects=True, vmem_limit_bytes=16 * 2**20),
    )(*(pltpu.with_memory_space_constraint(a, pltpu.HBM) for a in args))


def write_kernel(gate, up, down, rows, o_gate, o_up, o_down, o_norm, norm, sem):
    pairs = ((gate, o_gate), (up, o_up), (down, o_down))
    copies = [pltpu.make_async_copy(a, b, sem.at[i]) for i, (a, b) in enumerate(pairs)]
    for copy in copies:
        copy.start()
    per = rows.shape[1]
    lane = lax.broadcasted_iota(jnp.int32, norm.shape, 1) // (LANES // per)
    line = rows[:, 0, :]
    for j in range(1, per):
        line = jnp.where(lane == j, rows[:, j, :], line)
    norm[...] = line.astype(norm.dtype)
    copy = pltpu.make_async_copy(norm, o_norm, sem.at[3])
    copy.start()
    copy.wait()
    for copy in copies:
        copy.wait()


def write_out(gate, up, down, rows):
    any_ = pl.BlockSpec(memory_space=pl.ANY)
    vmem = pl.BlockSpec(memory_space=pltpu.VMEM)
    norm = (rows.shape[0], LANES)
    return pl.pallas_call(
        write_kernel,
        out_shape=tuple(jax.ShapeDtypeStruct(a.shape, a.dtype) for a in (gate, up, down))
        + (jax.ShapeDtypeStruct(norm, jnp.bfloat16),),
        in_specs=[any_] * 3 + [vmem],
        out_specs=(any_,) * 4,
        scratch_shapes=[pltpu.VMEM(norm, jnp.bfloat16), pltpu.SemaphoreType.DMA((4,))],
        compiler_params=pltpu.CompilerParams(vmem_limit_bytes=4 * 2**20),
    )(gate, up, down, rows)


def body(
    shards,
    widths,
    w_gate,
    low_gate,
    high_gate,
    w_up,
    low_up,
    high_up,
    w_down,
    low_down,
    high_down,
    norm_train,
    norm_step,
):
    count = norm_train.shape[0]
    wide, tall = w_gate.shape
    if shards % X or wide % LANES or tall % (CUTS * LANES) or LANES % count or (shards * widths * count) % LANES:
        gate = merged(w_gate, low_gate, high_gate)
        up = merged(w_up, low_up, high_up)
        down = merged(w_down, low_down, high_down)
        gate, up, down = (
            lax.all_gather(gate, "shard", axis=0, tiled=True),
            lax.all_gather(up, "shard", axis=0, tiled=True),
            lax.all_gather(down, "shard", axis=1, tiled=True),
        )
        gain = (norm_train + norm_step).astype(jnp.bfloat16)
        gain = lax.all_gather(gain, ("shard", "width"), axis=0, tiled=True)
        return gate.T, up.T, down.T, gain
    args = (
        w_gate, low_gate.T, high_gate, w_up, low_up.T, high_up, w_down, low_down.T, high_down,
        norm_train.reshape(1, count), norm_step.reshape(1, count),
    )
    gate, up, down, rows = gather_all(shards, widths, args)
    per = LANES // count
    gate, up, down, norm = write_out(gate, up, down, rows.reshape(-1, per, LANES))
    return gate, up, down, norm.reshape(-1)


def solution(mesh):
    return jax.shard_map(
        functools.partial(body, mesh.shape["shard"], mesh.shape["width"]),
        mesh=mesh,
        in_specs=(
            P("shard", "width"),
            P("shard", None),
            P(None, "width"),
            P("shard", "width"),
            P("shard", None),
            P(None, "width"),
            P("width", "shard"),
            P("width", None),
            P(None, "shard"),
            P(("shard", "width")),
            P(("shard", "width")),
        ),
        out_specs=(P("width", None), P("width", None), P(None, "width"), P()),
        check_vma=False,
    )
```

time: 267 us -> 269 us (level)
  Pallas kernels: 256 us -> 268 us
  local copies, waits for them, and re-layouts: 6.1 us -> 0 us
  matrix products: 3.38 us -> 0 us
    pallas_call x1, Pallas kernels: 247 us -> 259 us  [gather_all(): pl.pallas_call(functools.partial(gather_kernel, shards, widths), out_shap...]
    unnamed x13 -> x0, local copies, waits for them, and re-layouts: 5.37 us -> none
    dot_general x3 -> x0, matrix products: 3.38 us -> none  [merged(): jnp.dot(low, high, preferred_element_type=jnp.float32)]
where the time goes in v1:
time: 269 us; the launch traced here: 268 us
  Pallas kernels  268 us (100%)
    pallas_call x1, Pallas kernels, gather_all(): pl.pallas_call(functools.partial(gather_kernel, shards, widths), out_shap...  259 us
    pallas_call x1, Pallas kernels, write_out(): pl.pallas_call(write_kernel, out_shape=tuple((jax.ShapeDtypeStruct(a.shap...  8.72 us

profile of v1, /device:TPU:0, one launch (start us, length us, event | category | flops | bytes accessed | tf_op | source)
XLA Modules:
  0.0 268.4 jit_solution(18343655186462595604)
XLA Ops:
  0.6 259.1 %shard_map.138 = (bf16[2048,2048]{1,0:T(8,128)(2,1)S(1)}, bf16[2048,2048]{1,0:T(8,128)(2,1)S(1)}, bf16[2048,2048]{1,0:T(8,128)(2,1)S(1)}, f32[32,1,128]{2,1,0:T(1,128)S(1)}) custom-call(bf16[256,2048]{1,0:T(8,128)(2,1)} %w_gate.1, bf16[64,256]{1,0:T(8,128)(2,1)} %bitcast.9, bf16[64,2048]{1,0:T(8,128)(2,1)} %high_gate.1, bf16[256,2048]{1,0:T(8,128)(2,1)} %w_up.1, ...), custom_call_target="tpu_custom_call" | custom-call | tf_op jit(solution)/shard_map/pallas_call | solution.py:283
  259.7 8.7 %shard_map.139 = (bf16[2048,2048]{1,0:T(8,128)(2,1)}, bf16[2048,2048]{1,0:T(8,128)(2,1)}, bf16[2048,2048]{1,0:T(8,128)(2,1)}, bf16[16,128]{1,0:T(8,128)(2,1)}) custom-call(bf16[2048,2048]{1,0:T(8,128)(2,1)S(1)} %get-tuple-element.12.gate, bf16[2048,2048]{1,0:T(8,128)(2,1)S(1)} %get-tuple-element.13.up, bf16[2048,2048]{1,0:T(8,128)(2,1)S(1)} %get-tuple-element.14.down, ...), custom_call_target="tpu_custom_call" | custom-call | tf_op jit(solution)/shard_map/pallas_call | solution.py:331

commit v2 on v1

v2 whole, which is shorter than its diff:
```python
import functools

import jax
import jax.numpy as jnp
from jax import lax
from jax.experimental import pallas as pl
from jax.experimental.pallas import tpu as pltpu
from jax.sharding import PartitionSpec as P

mix_rate = 2.0
MESH = pl.DeviceIdType.MESH
X = 2
LANES = 128

UNITS = 16
LINE = ((0, 0, 1), (0, 1, 3), (0, 4, 12), (1, 0, 8), (2, 0, 8), (2, 8, 8))
PAIR = ((1, 8, 8),)
ORDER = LINE[:3] + PAIR + LINE[3:]
UP, DOWN, SIDE = 0, 1, 2
WAYS = 3
WRITES = 4


def units_of(pieces, t):
    return sum(n for array, _, n in pieces if array == t)


def merged(w, low, high):
    fresh = w.astype(jnp.float32) + mix_rate * jnp.dot(
        low, high, preferred_element_type=jnp.float32
    )
    return fresh.astype(jnp.bfloat16)


def when(cond, fn):
    if cond is None:
        fn()
    else:
        pl.when(cond)(fn)


def both(a, b):
    if a is None:
        return b
    if b is None:
        return a
    return jnp.logical_and(a, b)


def gather_kernel(
    shards, widths,
    w_gate, low_gate, high_gate, w_up, low_up, high_up, w_down, low_down, high_down, train, step,
    o_gate, o_up, o_down, o_norm,
    v_gate, v_up, v_down, v_low_gate, v_low_up, v_low_down, v_high_gate, v_high_up, v_high_down,
    v_train, v_step, l_gate, l_up, h_down,
    send_sem, line_sem, pair_sem, side_sem, norm_send, norm_recv, load_sem, small_sem,
):
    lines = shards // X
    me, w = lax.axis_index("shard"), lax.axis_index("width")
    z, x = me // X, me % X
    partner = z * X + (1 - x)
    outs = (o_gate, o_up, o_down)
    wide, tall = w_gate.shape
    unit = tall // UNITS

    head = LINE[0][2] * unit
    loads = [
        pltpu.make_async_copy(w_gate.at[:, pl.ds(0, head)], v_gate.at[:, pl.ds(0, head)], load_sem.at[0]),
        pltpu.make_async_copy(w_gate.at[:, pl.ds(head, tall - head)], v_gate.at[:, pl.ds(head, tall - head)], load_sem.at[1]),
        pltpu.make_async_copy(w_up, v_up, load_sem.at[2]),
        pltpu.make_async_copy(w_down, v_down, load_sem.at[3]),
    ]
    smalls = (
        (low_gate, v_low_gate), (high_gate, v_high_gate),
        (low_up, v_low_up), (high_up, v_high_up),
        (low_down, v_low_down), (high_down, v_high_down),
        (train, v_train), (step, v_step),
    )
    small = [pltpu.make_async_copy(a, b, small_sem.at[i]) for i, (a, b) in enumerate(smalls)]
    for copy in small[:2] + loads[:2] + small[2:4] + loads[2:3] + small[4:6] + loads[3:] + small[6:]:
        copy.start()

    def target(way):
        return {UP: me + X, DOWN: me - X, SIDE: partner}[way]

    def has(way):
        return {UP: z + 1 < lines, DOWN: z > 0, SIDE: None}[way]

    barrier = pltpu.get_barrier_semaphore()
    peers = [lax.rem(w + k, widths) for k in range(1, widths)]
    for way in (UP, DOWN, SIDE):
        when(
            has(way),
            lambda way=way: pl.semaphore_signal(
                barrier, inc=1, device_id=(target(way), w), device_id_type=MESH
            ),
        )
    for p in peers:
        pl.semaphore_signal(barrier, inc=1, device_id=(me, p), device_id_type=MESH)

    def place(s, c):
        t, first, n = c
        block = pl.ds(pl.multiple_of(s * wide, wide), wide)
        inner = pl.ds(first * unit, n * unit)
        return outs[t].at[inner, block] if t < 2 else outs[t].at[block, inner]

    def receipt(way, s, c):
        if c in PAIR:
            return pair_sem.at[s * len(PAIR) + PAIR.index(c)]
        return side_sem.at[c[0]] if way == SIDE else line_sem.at[s // X * len(LINE) + LINE.index(c)]

    def remote(way, s, c):
        return pltpu.make_async_remote_copy(
            src_ref=place(s, c),
            dst_ref=place(s, c),
            send_sem=send_sem.at[way * len(outs) + c[0]],
            recv_sem=receipt(way, s, c),
            device_id=(target(way), w),
            device_id_type=MESH,
        )

    def send(way, s, c, cond=None):
        when(both(cond, has(way)), lambda: remote(way, s, c).start())

    def arrive(way, s, c, cond=None):
        when(cond, lambda: remote(way, s, c).wait_recv())

    def bulk(t, elements):
        return outs[t].at[pl.ds(0, elements // outs[t].shape[1])]

    def drain(way, t, units):
        ref = bulk(t, units * unit * wide)
        pltpu.make_async_remote_copy(
            src_ref=ref, dst_ref=ref, send_sem=send_sem.at[way * len(outs) + t], recv_sem=side_sem.at[t],
            device_id=(partner, w), device_id_type=MESH,
        ).wait_send()

    def collect(t, units):
        ref = bulk(t, units * unit * wide)
        pltpu.make_async_remote_copy(
            src_ref=ref, dst_ref=ref, send_sem=send_sem.at[t], recv_sem=side_sem.at[t],
            device_id=(partner, w), device_id_type=MESH,
        ).wait_recv()

    waits = {LINE[0]: loads[:1], LINE[1]: loads[1:2]}
    seen = set()

    def compute(c):
        t, first, n = c
        pending = waits.get(c, [])
        if t not in seen:
            seen.add(t)
            pending = small[2 * t : 2 * t + 2] + (pending if t == 0 else loads[t + 1 : t + 2])
        for copy in pending:
            copy.wait()
        if len(pending) > 1:
            if t == 0:
                l_gate[...] = v_low_gate[...].T
            elif t == 1:
                l_up[...] = v_low_up[...].T
            else:
                h_down[...] = v_high_down[...].T
        columns = pl.ds(pl.multiple_of(me * wide, wide), wide)

        @pl.loop(0, n * unit // LANES)
        def _(i):
            at = pl.ds(pl.multiple_of(first * unit + i * LANES, LANES), LANES)
            if t < 2:
                block, low, high = ((v_gate, l_gate, v_high_gate), (v_up, l_up, v_high_up))[t]
                outs[t][at, columns] = merged(block[:, at], low[...], high[:, at]).T
            else:
                o_down[columns, at] = merged(v_down[at, :].T, h_down[...], v_low_down[:, at])

    compute(ORDER[0])
    inner = jnp.logical_and(z > 0, z + 1 < lines)
    pl.when(inner)(lambda: pl.semaphore_wait(barrier, widths + 2))
    ends = widths + (1 if lines > 1 else 0)
    pl.when(jnp.logical_not(inner))(lambda: pl.semaphore_wait(barrier, ends))
    for k, c in enumerate(ORDER):
        if k:
            compute(c)
        if c in LINE:
            send(UP, me, c)
            send(DOWN, me, c)
        send(SIDE, me, c)

    def norm_rows(begin, count):
        return o_norm.at[pl.ds(begin, count)]

    def norm_copy(begin, count, sem, rsem, dev):
        return pltpu.make_async_remote_copy(
            src_ref=norm_rows(begin, count), dst_ref=norm_rows(begin, count),
            send_sem=norm_send.at[sem], recv_sem=norm_recv.at[rsem],
            device_id=dev, device_id_type=MESH,
        )

    for copy in small[6:]:
        copy.wait()
    gain = v_train[...] + v_step[...]
    row = jnp.concatenate([gain] * (LANES // gain.shape[1]), axis=1)
    o_norm[pl.ds(me * widths + w, 1)] = row.reshape(1, 1, LANES)
    for p in peers:
        norm_copy(me * widths + w, 1, 3, 0, (me, p)).start()
    tiles = lambda: norm_copy(0, widths - 1, 3, 0, (partner, w))
    norm_side = lambda s: norm_copy(s * widths, widths, SIDE, 1, (partner, w))
    plane_rows = X * widths
    norm_plane = lambda way, plane: norm_copy(plane * plane_rows, plane_rows, way, 2 + plane, (target(way), w))
    if widths > 1:
        tiles().wait_recv()
    norm_side(me).start()

    def hops(d):
        return ((UP, z - d, z >= d), (DOWN, z + d, z + d < lines))

    def forward_line(d):
        for c in LINE:
            for way, plane, cond in hops(d):
                s = plane * X + x
                arrive(way, s, c, cond)
                send(way, s, c, cond)
                send(SIDE, s, c, cond)

    def forward_pair(d):
        if d == 0:
            for c in PAIR:
                send(UP, me, c)
                send(DOWN, me, c)
            norm_side(partner).wait_recv()
            for way in (UP, DOWN):
                when(has(way), lambda way=way: norm_plane(way, z).start())
            for c in PAIR:
                arrive(SIDE, partner, c)
                send(UP, partner, c)
                send(DOWN, partner, c)
            return
        for way, plane, cond in hops(d):
            when(cond, lambda way=way, plane=plane: norm_plane(way, plane).wait_recv())
            when(both(cond, has(way)), lambda way=way, plane=plane: norm_plane(way, plane).start())
        for c in PAIR:
            for j in range(X):
                for way, plane, cond in hops(d):
                    s = plane * X + (x + j) % X
                    arrive(way, s, c, cond)
                    send(way, s, c, cond)

    for d in range(1, lines):
        forward_line(d)
        forward_pair(d - 1)
    forward_pair(lines - 1)

    for t in range(len(outs)):
        collect(t, lines * units_of(LINE, t))
        drain(SIDE, t, lines * units_of(LINE, t) + units_of(PAIR, t))
    norm_side(me).wait_send()
    if widths > 1:
        tiles().wait_send()
    for way in (UP, DOWN):
        for k in range(lines):
            planes = k + 1 if way == UP else lines - k

            @pl.when(both(z == k, has(way)))
            def _(way=way, planes=planes):
                for t in range(len(outs)):
                    drain(way, t, planes * (units_of(LINE, t) + X * units_of(PAIR, t)))
                norm_copy(0, planes * plane_rows, way, 0, (partner, w)).wait_send()


def gather_all(shards, widths, args):
    lines = shards // X
    w_gate, low_gate, high_gate, w_up, low_up, high_up, w_down, low_down, high_down, train, step = args
    hbm = pl.BlockSpec(memory_space=pltpu.HBM)
    vmem = pl.BlockSpec(memory_space=pltpu.VMEM)
    like = lambda a: pltpu.VMEM(a.shape, a.dtype)
    flip = lambda a: pltpu.VMEM(a.shape[::-1], a.dtype)
    wide, tall = w_gate.shape
    full = pltpu.VMEM((tall, shards * wide), w_gate.dtype)
    return pl.pallas_call(
        functools.partial(gather_kernel, shards, widths),
        out_shape=(
            full, full,
            pltpu.VMEM((shards * wide, tall), w_down.dtype),
            pltpu.VMEM((shards * widths, 1, LANES), train.dtype),
        ),
        in_specs=[hbm] * len(args),
        out_specs=(vmem,) * 4,
        scratch_shapes=[
            like(w_gate), like(w_up), like(w_down),
            like(low_gate), like(low_up), like(low_down),
            like(high_gate), like(high_up), like(high_down),
            like(train), like(step),
            flip(low_gate), flip(low_up), flip(high_down),
            pltpu.SemaphoreType.DMA((WAYS * 3,)),
            pltpu.SemaphoreType.DMA((lines * len(LINE),)),
            pltpu.SemaphoreType.DMA((shards * len(PAIR),)),
            pltpu.SemaphoreType.DMA((3,)),
            pltpu.SemaphoreType.DMA((4,)),
            pltpu.SemaphoreType.DMA((2 + lines,)),
            pltpu.SemaphoreType.DMA((4,)),
            pltpu.SemaphoreType.DMA((8,)),
        ],
        compiler_params=pltpu.CompilerParams(collective_id=0, has_side_effects=True, vmem_limit_bytes=16 * 2**20),
    )(*(pltpu.with_memory_space_constraint(a, pltpu.HBM) for a in args))


def write_kernel(gate, up, down, rows, o_gate, o_up, o_down, o_norm, norm, sem):
    pairs = ((gate, o_gate), (up, o_up), (down, o_down))
    part = gate.shape[0] // WRITES
    copies = [
        pltpu.make_async_copy(a.at[pl.ds(j * part, part)], b.at[pl.ds(j * part, part)], sem.at[i * WRITES + j])
        for i, (a, b) in enumerate(pairs)
        for j in range(WRITES)
    ]
    for copy in copies:
        copy.start()
    per = rows.shape[1]
    lane = lax.broadcasted_iota(jnp.int32, norm.shape, 1) // (LANES // per)
    line = rows[:, 0, :]
    for j in range(1, per):
        line = jnp.where(lane == j, rows[:, j, :], line)
    norm[...] = line.astype(norm.dtype)
    last = pltpu.make_async_copy(norm, o_norm, sem.at[len(copies)])
    last.start()
    for copy in copies:
        copy.wait()
    last.wait()


def write_out(gate, up, down, rows):
    any_ = pl.BlockSpec(memory_space=pl.ANY)
    vmem = pl.BlockSpec(memory_space=pltpu.VMEM)
    norm = (rows.shape[0], LANES)
    return pl.pallas_call(
        write_kernel,
        out_shape=tuple(jax.ShapeDtypeStruct(a.shape, a.dtype) for a in (gate, up, down))
        + (jax.ShapeDtypeStruct(norm, jnp.bfloat16),),
        in_specs=[any_] * 3 + [vmem],
        out_specs=(any_,) * 4,
        scratch_shapes=[pltpu.VMEM(norm, jnp.bfloat16), pltpu.SemaphoreType.DMA((3 * WRITES + 1,))],
        compiler_params=pltpu.CompilerParams(vmem_limit_bytes=4 * 2**20),
    )(gate, up, down, rows)


def body(
    shards,
    widths,
    w_gate,
    low_gate,
    high_gate,
    w_up,
    low_up,
    high_up,
    w_down,
    low_down,
    high_down,
    norm_train,
    norm_step,
):
    count = norm_train.shape[0]
    wide, tall = w_gate.shape
    if shards % X or wide % LANES or tall % (UNITS * LANES) or LANES % count or (shards * widths * count) % LANES:
        gate = merged(w_gate, low_gate, high_gate)
        up = merged(w_up, low_up, high_up)
        down = merged(w_down, low_down, high_down)
        gate, up, down = (
            lax.all_gather(gate, "shard", axis=0, tiled=True),
            lax.all_gather(up, "shard", axis=0, tiled=True),
            lax.all_gather(down, "shard", axis=1, tiled=True),
        )
        gain = (norm_train + norm_step).astype(jnp.bfloat16)
        gain = lax.all_gather(gain, ("shard", "width"), axis=0, tiled=True)
        return gate.T, up.T, down.T, gain
    args = (
        w_gate, low_gate.T, high_gate, w_up, low_up.T, high_up, w_down, low_down.T, high_down,
        norm_train.reshape(1, count), norm_step.reshape(1, count),
    )
    gate, up, down, rows = gather_all(shards, widths, args)
    per = LANES // count
    gate, up, down, norm = write_out(gate, up, down, rows.reshape(-1, per, LANES))
    return gate, up, down, norm.reshape(-1)


def solution(mesh):
    return jax.shard_map(
        functools.partial(body, mesh.shape["shard"], mesh.shape["width"]),
        mesh=mesh,
        in_specs=(
            P("shard", "width"),
            P("shard", None),
            P(None, "width"),
            P("shard", "width"),
            P("shard", None),
            P(None, "width"),
            P("width", "shard"),
            P("width", None),
            P(None, "shard"),
            P(("shard", "width")),
            P(("shard", "width")),
        ),
        out_specs=(P("width", None), P("width", None), P(None, "width"), P()),
        check_vma=False,
    )
```

time: 269 us -> 252 us (0.937)
  Pallas kernels: 268 us -> 251 us
    pallas_call x1, Pallas kernels: 259 us -> 242 us  [gather_all(): pl.pallas_call(functools.partial(gather_kernel, shards, widths), out_shap...]
where the time goes in v2:
time: 252 us
  Pallas kernels  251 us (100%)
    pallas_call x1, Pallas kernels, gather_all(): pl.pallas_call(functools.partial(gather_kernel, shards, widths), out_shap...  242 us
    pallas_call x1, Pallas kernels, write_out(): pl.pallas_call(write_kernel, out_shape=tuple((jax.ShapeDtypeStruct(a.shap...  8.49 us

profile of v2, /device:TPU:0, one launch (start us, length us, event | category | flops | bytes accessed | tf_op | source)
XLA Modules:
  0.0 251.6 jit_solution(8601077379117003950)
XLA Ops:
  0.6 242.5 %shard_map.138 = (bf16[2048,2048]{1,0:T(8,128)(2,1)S(1)}, bf16[2048,2048]{1,0:T(8,128)(2,1)S(1)}, bf16[2048,2048]{1,0:T(8,128)(2,1)S(1)}, f32[32,1,128]{2,1,0:T(1,128)S(1)}) custom-call(bf16[256,2048]{1,0:T(8,128)(2,1)} %w_gate.1, bf16[64,256]{1,0:T(8,128)(2,1)} %bitcast.9, bf16[64,2048]{1,0:T(8,128)(2,1)} %high_gate.1, bf16[256,2048]{1,0:T(8,128)(2,1)} %w_up.1, ...), custom_call_target="tpu_custom_call" | custom-call | tf_op jit(solution)/shard_map/pallas_call | solution.py:277
  243.1 8.5 %shard_map.139 = (bf16[2048,2048]{1,0:T(8,128)(2,1)}, bf16[2048,2048]{1,0:T(8,128)(2,1)}, bf16[2048,2048]{1,0:T(8,128)(2,1)}, bf16[16,128]{1,0:T(8,128)(2,1)}) custom-call(bf16[2048,2048]{1,0:T(8,128)(2,1)S(1)} %get-tuple-element.12.gate, bf16[2048,2048]{1,0:T(8,128)(2,1)S(1)} %get-tuple-element.13.up, bf16[2048,2048]{1,0:T(8,128)(2,1)S(1)} %get-tuple-element.14.down, ...), custom_call_target="tpu_custom_call" | custom-call | tf_op jit(solution)/shard_map/pallas_call | solution.py:332

commit v3 on v2

--- a/solution.py
+++ b/solution.py
@@ -13,12 +13,14 @@
 LANES = 128
 
 UNITS = 16
-LINE = ((0, 0, 1), (0, 1, 3), (0, 4, 12), (1, 0, 8), (2, 0, 8), (2, 8, 8))
-PAIR = ((1, 8, 8),)
+LINE = ((0, 0, 1), (0, 1, 3), (0, 4, 12), (1, 0, 8), (2, 0, 8), (2, 8, 3), (2, 11, 5))
+PAIR = ((1, 8, 3), (1, 11, 5))
+LATE_LINE, LATE_PAIR = LINE[-1], PAIR[-1]
 ORDER = LINE[:3] + PAIR + LINE[3:]
 UP, DOWN, SIDE = 0, 1, 2
 WAYS = 3
 WRITES = 4
+WRITE_FLOPS = 2 * 10**9
 
 
 def units_of(pieces, t):
@@ -47,10 +49,14 @@
     return jnp.logical_and(a, b)
 
 
+def far_plane(z, lines):
+    return jnp.where(z < lines // 2, lines - 1, 0)
+
+
 def gather_kernel(
     shards, widths,
     w_gate, low_gate, high_gate, w_up, low_up, high_up, w_down, low_down, high_down, train, step,
-    o_gate, o_up, o_down, o_norm,
+    o_gate, o_up, o_down, o_norm, late_x, late_z,
     v_gate, v_up, v_down, v_low_gate, v_low_up, v_low_down, v_high_gate, v_high_up, v_high_down,
     v_train, v_step, l_gate, l_up, h_down,
     send_sem, line_sem, pair_sem, side_sem, norm_send, norm_recv, load_sem, small_sem,
@@ -209,6 +215,8 @@
         tiles().wait_recv()
     norm_side(me).start()
 
+    far = far_plane(z, lines)
+
     def hops(d):
         return ((UP, z - d, z >= d), (DOWN, z + d, z + d < lines))
 
@@ -218,7 +226,23 @@
                 s = plane * X + x
                 arrive(way, s, c, cond)
                 send(way, s, c, cond)
-                send(SIDE, s, c, cond)
+                send(SIDE, s, c, both(cond, plane != far) if c == LATE_LINE else cond)
+
+    source = {UP: 0, DOWN: lines - 1}
+    feeds = {UP: z == lines - 2, DOWN: z == 1}
+
+    def send_pair(way, plane, j, c, cond=None):
+        if c == LATE_PAIR and j == 1:
+            late = jnp.logical_and(feeds[way], plane == source[way])
+            cond = both(cond, jnp.logical_not(late))
+        send(way, plane * X + (x + j) % X, c, cond)
+
+    def arrive_pair(way, plane, j, c, cond):
+        if c == LATE_PAIR and j == 1:
+            end = {UP: z == lines - 1, DOWN: z == 0}[way]
+            late = jnp.logical_and(end, plane == source[way])
+            cond = both(cond, jnp.logical_not(late))
+        arrive(way, plane * X + (x + j) % X, c, cond)
 
     def forward_pair(d):
         if d == 0:
@@ -230,8 +254,8 @@
                 when(has(way), lambda way=way: norm_plane(way, z).start())
             for c in PAIR:
                 arrive(SIDE, partner, c)
-                send(UP, partner, c)
-                send(DOWN, partner, c)
+                send_pair(UP, z, 1, c)
+                send_pair(DOWN, z, 1, c)
             return
         for way, plane, cond in hops(d):
             when(cond, lambda way=way, plane=plane: norm_plane(way, plane).wait_recv())
@@ -239,18 +263,23 @@
         for c in PAIR:
             for j in range(X):
                 for way, plane, cond in hops(d):
-                    s = plane * X + (x + j) % X
-                    arrive(way, s, c, cond)
-                    send(way, s, c, cond)
+                    arrive_pair(way, plane, j, c, cond)
+                    send_pair(way, plane, j, c, cond)
 
     for d in range(1, lines):
         forward_line(d)
         forward_pair(d - 1)
+    bridge = jnp.logical_or(z == 1, z == lines - 2)
+    keep = jnp.where(z == 1, lines - 1, 0) * X + (1 - x)
+    keep = jnp.where(bridge, keep, me)
+    late_x[...] = place(far * X + x, LATE_LINE)[...]
+    late_z[...] = place(keep, LATE_PAIR)[...]
     forward_pair(lines - 1)
 
     for t in range(len(outs)):
-        collect(t, lines * units_of(LINE, t))
-        drain(SIDE, t, lines * units_of(LINE, t) + units_of(PAIR, t))
+        skipped = LATE_LINE[2] * (t == LATE_LINE[0])
+        collect(t, lines * units_of(LINE, t) - skipped)
+        drain(SIDE, t, lines * units_of(LINE, t) + units_of(PAIR, t) - skipped)
     norm_side(me).wait_send()
     if widths > 1:
         tiles().wait_send()
@@ -260,8 +289,10 @@
 
             @pl.when(both(z == k, has(way)))
             def _(way=way, planes=planes):
+                feeder = k == (lines - 2 if way == UP else 1)
                 for t in range(len(outs)):
-                    drain(way, t, planes * (units_of(LINE, t) + X * units_of(PAIR, t)))
+                    skipped = LATE_PAIR[2] * (feeder and t == LATE_PAIR[0])
+                    drain(way, t, planes * (units_of(LINE, t) + X * units_of(PAIR, t)) - skipped)
                 norm_copy(0, planes * plane_rows, way, 0, (partner, w)).wait_send()
 
 
@@ -280,9 +311,11 @@
             full, full,
             pltpu.VMEM((shards * wide, tall), w_down.dtype),
             pltpu.VMEM((shards * widths, 1, LANES), train.dtype),
+            pltpu.VMEM((wide, LATE_LINE[2] * tall // UNITS), w_down.dtype),
+            pltpu.VMEM((LATE_PAIR[2] * tall // UNITS, wide), w_up.dtype),
         ),
         in_specs=[hbm] * len(args),
-        out_specs=(vmem,) * 4,
+        out_specs=(vmem,) * 6,
         scratch_shapes=[
             like(w_gate), like(w_up), like(w_down),
             like(low_gate), like(low_up), like(low_down),
@@ -336,8 +369,53 @@
         in_specs=[any_] * 3 + [vmem],
         out_specs=(any_,) * 4,
         scratch_shapes=[pltpu.VMEM(norm, jnp.bfloat16), pltpu.SemaphoreType.DMA((3 * WRITES + 1,))],
+        cost_estimate=pl.CostEstimate(flops=WRITE_FLOPS, bytes_accessed=2 * 3 * gate.size * 2, transcendentals=0),
         compiler_params=pltpu.CompilerParams(vmem_limit_bytes=4 * 2**20),
     )(gate, up, down, rows)
+
+
+def late_kernel(lines, up, down, late_x, late_z, o_up, o_down, v_x, v_z, sem):
+    me = lax.axis_index("shard")
+    z, x = me // X, me % X
+    wide, tall = late_z.shape[1], up.shape[0]
+    unit = tall // UNITS
+    end = jnp.logical_or(z == 0, z == lines - 1)
+    block = (far_plane(z, lines) * X + (1 - x)) * wide
+    block = pl.ds(pl.multiple_of(block, wide), wide)
+    inner = lambda c: pl.ds(c[1] * unit, c[2] * unit)
+    get_x = pltpu.make_async_copy(late_x, v_x, sem.at[0])
+    get_z = pltpu.make_async_copy(late_z, v_z, sem.at[1])
+    put_x = pltpu.make_async_copy(v_x, o_down.at[block, inner(LATE_LINE)], sem.at[2])
+    put_z = pltpu.make_async_copy(v_z, o_up.at[inner(LATE_PAIR), block], sem.at[3])
+    get_x.start()
+    pl.when(end)(get_z.start)
+    get_x.wait()
+    put_x.start()
+
+    @pl.when(end)
+    def _():
+        get_z.wait()
+        put_z.start()
+        put_z.wait()
+
+    put_x.wait()
+
+
+def write_late(lines, up, down, late_x, late_z):
+    any_ = pl.BlockSpec(memory_space=pl.ANY)
+    return pl.pallas_call(
+        functools.partial(late_kernel, lines),
+        out_shape=tuple(jax.ShapeDtypeStruct(a.shape, a.dtype) for a in (up, down)),
+        in_specs=[any_] * 4,
+        out_specs=(any_,) * 2,
+        input_output_aliases={0: 0, 1: 1},
+        scratch_shapes=[
+            pltpu.VMEM(late_x.shape, late_x.dtype),
+            pltpu.VMEM(late_z.shape, late_z.dtype),
+            pltpu.SemaphoreType.DMA((4,)),
+        ],
+        compiler_params=pltpu.CompilerParams(vmem_limit_bytes=4 * 2**20),
+    )(up, down, late_x, late_z)
 
 
 def body(
@@ -357,7 +435,7 @@
 ):
     count = norm_train.shape[0]
     wide, tall = w_gate.shape
-    if shards % X or wide % LANES or tall % (UNITS * LANES) or LANES % count or (shards * widths * count) % LANES:
+    if shards % (2 * X) or wide % LANES or tall % (UNITS * LANES) or LANES % count or (shards * widths * count) % LANES:
         gate = merged(w_gate, low_gate, high_gate)
         up = merged(w_up, low_up, high_up)
         down = merged(w_down, low_down, high_down)
@@ -373,9 +451,12 @@
         w_gate, low_gate.T, high_gate, w_up, low_up.T, high_up, w_down, low_down.T, high_down,
         norm_train.reshape(1, count), norm_step.reshape(1, count),
     )
-    gate, up, down, rows = gather_all(shards, widths, args)
+    gate, up, down, rows, late_x, late_z = gather_all(shards, widths, args)
     per = LANES // count
+    late_x = lax.ppermute(late_x, "shard", [(s, s ^ 1) for s in range(shards)])
+    late_z = lax.ppermute(late_z, "shard", [(s, s ^ X) for s in range(shards)])
     gate, up, down, norm = write_out(gate, up, down, rows.reshape(-1, per, LANES))
+    up, down = write_late(shards // X, up, down, late_x, late_z)
     return gate, up, down, norm.reshape(-1)
 
 

time: 252 us -> 248 us (0.984)
  Pallas kernels: 251 us -> 245 us
    pallas_call x1, Pallas kernels: 242 us -> 236 us  [gather_all(): pl.pallas_call(functools.partial(gather_kernel, shards, widths), out_shap...]
  transfers between devices with their start and end apart: 0 -> 2, of which waited for: 0 -> 0; matrix products, arithmetic and copies ran while one was open for 0% -> 0% of each run, Pallas kernels for 0% -> 3%
where the time goes in v3:
time: 248 us
  Pallas kernels  245 us (99%)
    pallas_call x1, Pallas kernels, gather_all(): pl.pallas_call(functools.partial(gather_kernel, shards, widths), out_shap...  236 us
    pallas_call x1, Pallas kernels, write_out(): pl.pallas_call(write_kernel, out_shape=tuple((jax.ShapeDtypeStruct(a.shap...  8.49 us
  transfers between devices with their start and end apart: 2, of which 0 were waited for; matrix products, arithmetic and copies ran while one was open for 0% of the time, Pallas kernels for 3%

profile of v3, /device:TPU:0, one launch (start us, length us, event | category | flops | bytes accessed | tf_op | source)
XLA Modules:
  0.0 247.7 jit_solution(12061660198514096792)
XLA Ops:
  0.6 235.6 %shard_map.138 = (bf16[2048,2048]{1,0:T(8,128)(2,1)S(1)}, bf16[2048,2048]{1,0:T(8,128)(2,1)S(1)}, bf16[2048,2048]{1,0:T(8,128)(2,1)S(1)}, f32[32,1,128]{2,1,0:T(...) custom-call(bf16[256,2048]{1,0:T(8,128)(2,1)} %w_gate.1, bf16[64,256]{1,0:T(8,128)(2,1)} %bitcast.9, ...), custom_call_target="tpu_custom_call" | custom-call | tf_op jit(solution)/shard_map/pallas_call | solution.py:308
  236.2 1.6 collective-permute-start
  237.8 0.3 collective-permute-start.1
  238.1 8.5 %shard_map.139 = (bf16[2048,2048]{1,0:T(8,128)(2,1)}, bf16[2048,2048]{1,0:T(8,128)(2,1)}, bf16[2048,2048]{1,0:T(8,128)(2,1)}, bf16[16,128]{1,0:T(8,128)(2,1)}) custom-call(bf16[2048,2048]{1,0:T(8,128)(2,1)S(1)} %get-tuple-element.16.gate, bf16[2048,2048]{1,0:T(8,128)(2,1)S(1)} %get-tuple-element.17.up, bf16[2048,2048]{1,0:T(8,128)(2,1)S(1)} %get-tuple-element.18.down, ...), custom_call_target="tpu_custom_call" | custom-call | flops 2000000000 | bytes 50331648 | tf_op jit(solution)/shard_map/pallas_call | solution.py:365
  246.6 0.0 collective-permute-done.late_x
  246.6 0.0 collective-permute-done.1.late_z
  246.6 1.1 shard_map.140
Async XLA Ops:
  236.2 10.3 %collective-permute-start = (bf16[256,640]{1,0:T(8,128)(2,1)S(1)}, bf16[256,640]{1,0:T(8,128)(2,1)S(1)}, u32[]{:S(2)}, u32[]{:S(2)}) collective-permute-start(bf16[256,640]{1,0:T(8,128)(2,1)S(1)} %get-tuple-element.23), channel_id=1, source_target_pairs={{0,4},{4,0},{8,12},{12,8},{16,20},{20,16},{24,28},{28,24},{1,5},{5... | collective-permute-start | bytes 983048 | tf_op jit(solution)/shard_map/ppermute | solution.py:456
  237.8 8.8 %collective-permute-start.1 = (bf16[640,256]{1,0:T(8,128)(2,1)S(1)}, bf16[640,256]{1,0:T(8,128)(2,1)S(1)}, u32[]{:S(2)}, u32[]{:S(2)}) collective-permute-start(bf16[640,256]{1,0:T(8,128)(2,1)S(1)} %get-tuple-element.24), channel_id=1, source_target_pairs={{0,8},{4,12},{8,0},{12,4},{16,24},{20,28},{24,16},{28,20},{1,9},{5... | collective-permute-start | bytes 983048 | tf_op jit(solution)/shard_map/ppermute | solution.py:457

commit v4 on v3

--- a/solution.py
+++ b/solution.py
@@ -13,11 +13,17 @@
 LANES = 128
 
 UNITS = 16
-LINE = ((0, 0, 1), (0, 1, 3), (0, 4, 12), (1, 0, 8), (2, 0, 8), (2, 8, 3), (2, 11, 5))
-PAIR = ((1, 8, 3), (1, 11, 5))
+LINE = ((0, 0, 16), (1, 0, 8), (2, 0, 10), (2, 10, 6))
+PAIR = ((1, 8, 2), (1, 10, 6))
+WHOLE = (1, 8, 8)
 LATE_LINE, LATE_PAIR = LINE[-1], PAIR[-1]
-ORDER = LINE[:3] + PAIR + LINE[3:]
+ORDER = (
+    ((0, 0, 1), LINE[0]), ((0, 1, 3), LINE[0]), ((0, 4, 12), LINE[0]),
+    (PAIR[0], PAIR[0]), (PAIR[1], PAIR[1]),
+    (LINE[1], LINE[1]), (LINE[2], LINE[2]), (LINE[3], LINE[3]),
+)
 UP, DOWN, SIDE = 0, 1, 2
+WIDE = DOWN
 WAYS = 3
 WRITES = 4
 WRITE_FLOPS = 2 * 10**9
@@ -59,7 +65,7 @@
     o_gate, o_up, o_down, o_norm, late_x, late_z,
     v_gate, v_up, v_down, v_low_gate, v_low_up, v_low_down, v_high_gate, v_high_up, v_high_down,
     v_train, v_step, l_gate, l_up, h_down,
-    send_sem, line_sem, pair_sem, side_sem, norm_send, norm_recv, load_sem, small_sem,
+    send_sem, line_sem, pair_sem, side_sem, norm_send, norm_recv, load_sem, small_sem, extra_sem, ready,
 ):
     lines = shards // X
     me, w = lax.axis_index("shard"), lax.axis_index("width")
@@ -69,7 +75,7 @@
     wide, tall = w_gate.shape
     unit = tall // UNITS
 
-    head = LINE[0][2] * unit
+    head = ORDER[0][0][2] * unit
     loads = [
         pltpu.make_async_copy(w_gate.at[:, pl.ds(0, head)], v_gate.at[:, pl.ds(0, head)], load_sem.at[0]),
         pltpu.make_async_copy(w_gate.at[:, pl.ds(head, tall - head)], v_gate.at[:, pl.ds(head, tall - head)], load_sem.at[1]),
@@ -94,15 +100,23 @@
 
     barrier = pltpu.get_barrier_semaphore()
     peers = [lax.rem(w + k, widths) for k in range(1, widths)]
-    for way in (UP, DOWN, SIDE):
-        when(
-            has(way),
-            lambda way=way: pl.semaphore_signal(
-                barrier, inc=1, device_id=(target(way), w), device_id_type=MESH
-            ),
-        )
-    for p in peers:
-        pl.semaphore_signal(barrier, inc=1, device_id=(me, p), device_id_type=MESH)
+    after = [w + k < widths for k in range(1, widths)]
+
+    def signal(sem, dev):
+        pl.semaphore_signal(sem, inc=1, device_id=dev, device_id_type=MESH)
+
+    when(has(UP), lambda: signal(barrier, (target(UP), w)))
+    pl.when(x == 0)(lambda: signal(barrier, (partner, w)))
+    for p, later in zip(peers, after):
+        pl.when(later)(lambda p=p: signal(barrier, (me, p)))
+
+    def enter():
+        before = jnp.where(z > 0, 1, 0) + x + w
+        pl.when(before > 0)(lambda: pl.semaphore_wait(barrier, before))
+        when(has(DOWN), lambda: signal(ready.at[UP], (target(DOWN), w)))
+        pl.when(x == 1)(lambda: signal(ready.at[SIDE], (partner, w)))
+        for p, later in zip(peers, after):
+            pl.when(jnp.logical_not(later))(lambda p=p: signal(ready.at[WIDE], (me, p)))
 
     def place(s, c):
         t, first, n = c
@@ -110,26 +124,30 @@
         inner = pl.ds(first * unit, n * unit)
         return outs[t].at[inner, block] if t < 2 else outs[t].at[block, inner]
 
-    def receipt(way, s, c):
-        if c in PAIR:
-            return pair_sem.at[s * len(PAIR) + PAIR.index(c)]
-        return side_sem.at[c[0]] if way == SIDE else line_sem.at[s // X * len(LINE) + LINE.index(c)]
-
-    def remote(way, s, c):
+    def receipt(way, s, whole, extra):
+        if whole == WHOLE:
+            return pair_sem.at[s // X * 3]
+        if whole in PAIR:
+            return pair_sem.at[s // X * 3 + 1 + PAIR.index(whole)]
+        if extra:
+            return extra_sem.at[0 if way == SIDE else 1]
+        return side_sem.at[whole[0]] if way == SIDE else line_sem.at[s // X * len(LINE) + LINE.index(whole)]
+
+    def remote(way, s, c, whole, extra=False):
         return pltpu.make_async_remote_copy(
             src_ref=place(s, c),
             dst_ref=place(s, c),
             send_sem=send_sem.at[way * len(outs) + c[0]],
-            recv_sem=receipt(way, s, c),
+            recv_sem=receipt(way, s, whole, extra),
             device_id=(target(way), w),
             device_id_type=MESH,
         )
 
-    def send(way, s, c, cond=None):
-        when(both(cond, has(way)), lambda: remote(way, s, c).start())
-
-    def arrive(way, s, c, cond=None):
-        when(cond, lambda: remote(way, s, c).wait_recv())
+    def send(way, s, c, cond=None, whole=None, extra=False):
+        when(both(cond, has(way)), lambda: remote(way, s, c, whole or c, extra).start())
+
+    def arrive(way, s, c, cond=None, extra=False):
+        when(cond, lambda: remote(way, s, c, c, extra).wait_recv())
 
     def bulk(t, elements):
         return outs[t].at[pl.ds(0, elements // outs[t].shape[1])]
@@ -148,7 +166,7 @@
             device_id=(partner, w), device_id_type=MESH,
         ).wait_recv()
 
-    waits = {LINE[0]: loads[:1], LINE[1]: loads[1:2]}
+    waits = {ORDER[0][0]: loads[:1], ORDER[1][0]: loads[1:2]}
     seen = set()
 
     def compute(c):
@@ -177,18 +195,24 @@
             else:
                 o_down[columns, at] = merged(v_down[at, :].T, h_down[...], v_low_down[:, at])
 
-    compute(ORDER[0])
-    inner = jnp.logical_and(z > 0, z + 1 < lines)
-    pl.when(inner)(lambda: pl.semaphore_wait(barrier, widths + 2))
-    ends = widths + (1 if lines > 1 else 0)
-    pl.when(jnp.logical_not(inner))(lambda: pl.semaphore_wait(barrier, ends))
-    for k, c in enumerate(ORDER):
-        if k:
-            compute(c)
-        if c in LINE:
-            send(UP, me, c)
-            send(DOWN, me, c)
-        send(SIDE, me, c)
+    def send_up(c, whole):
+        if whole in LINE:
+            send(UP, me, c, None, whole)
+
+    for k, (c, whole) in enumerate(ORDER):
+        compute(c)
+        if k == 0:
+            enter()
+        if k == 1:
+            when(has(UP), lambda: pl.semaphore_wait(ready.at[UP], 1))
+            send_up(*ORDER[0])
+        if whole in LINE:
+            send(DOWN, me, c, None, whole)
+        if k == 0:
+            pl.when(x == 0)(lambda: pl.semaphore_wait(ready.at[SIDE], 1))
+        else:
+            send_up(c, whole)
+        send(SIDE, me, c, None, whole, c == LATE_LINE)
 
     def norm_rows(begin, count):
         return o_norm.at[pl.ds(begin, count)]
@@ -205,6 +229,7 @@
     gain = v_train[...] + v_step[...]
     row = jnp.concatenate([gain] * (LANES // gain.shape[1]), axis=1)
     o_norm[pl.ds(me * widths + w, 1)] = row.reshape(1, 1, LANES)
+    pl.when(w + 1 < widths)(lambda: pl.semaphore_wait(ready.at[WIDE], widths - 1 - w))
     for p in peers:
         norm_copy(me * widths + w, 1, 3, 0, (me, p)).start()
     tiles = lambda: norm_copy(0, widths - 1, 3, 0, (partner, w))
@@ -216,6 +241,21 @@
     norm_side(me).start()
 
     far = far_plane(z, lines)
+    inner = jnp.logical_and(z > 0, z + 1 < lines)
+    lower = z < lines // 2
+    mate = jnp.where(lower, z + 1, z - 1)
+    lends = {
+        DOWN: jnp.logical_and(z >= 2, z - 1 < lines // 2),
+        UP: jnp.logical_and(z + 1 >= lines // 2, z + 2 < lines),
+    }
+
+    def by_side(plane):
+        return jnp.logical_and(plane != far, jnp.logical_not(jnp.logical_and(inner, plane == mate)))
+
+    def lend():
+        arrive(SIDE, partner, LATE_LINE, None, True)
+        for way in (UP, DOWN):
+            send(way, partner, LATE_LINE, lends[way], None, True)
 
     def hops(d):
         return ((UP, z - d, z >= d), (DOWN, z + d, z + d < lines))
@@ -226,19 +266,19 @@
                 s = plane * X + x
                 arrive(way, s, c, cond)
                 send(way, s, c, cond)
-                send(SIDE, s, c, both(cond, plane != far) if c == LATE_LINE else cond)
+                send(SIDE, s, c, both(cond, by_side(plane)) if c == LATE_LINE else cond)
 
     source = {UP: 0, DOWN: lines - 1}
     feeds = {UP: z == lines - 2, DOWN: z == 1}
 
     def send_pair(way, plane, j, c, cond=None):
-        if c == LATE_PAIR and j == 1:
+        if c == LATE_PAIR:
             late = jnp.logical_and(feeds[way], plane == source[way])
             cond = both(cond, jnp.logical_not(late))
         send(way, plane * X + (x + j) % X, c, cond)
 
     def arrive_pair(way, plane, j, c, cond):
-        if c == LATE_PAIR and j == 1:
+        if c == LATE_PAIR:
             end = {UP: z == lines - 1, DOWN: z == 0}[way]
             late = jnp.logical_and(end, plane == source[way])
             cond = both(cond, jnp.logical_not(late))
@@ -246,9 +286,8 @@
 
     def forward_pair(d):
         if d == 0:
-            for c in PAIR:
-                send(UP, me, c)
-                send(DOWN, me, c)
+            send(UP, me, WHOLE)
+            send(DOWN, me, WHOLE)
             norm_side(partner).wait_recv()
             for way in (UP, DOWN):
                 when(has(way), lambda way=way: norm_plane(way, z).start())
@@ -260,8 +299,8 @@
         for way, plane, cond in hops(d):
             when(cond, lambda way=way, plane=plane: norm_plane(way, plane).wait_recv())
             when(both(cond, has(way)), lambda way=way, plane=plane: norm_plane(way, plane).start())
-        for c in PAIR:
-            for j in range(X):
+        for j, pieces in enumerate(((WHOLE,), PAIR)):
+            for c in pieces:
                 for way, plane, cond in hops(d):
                     arrive_pair(way, plane, j, c, cond)
                     send_pair(way, plane, j, c, cond)
@@ -269,6 +308,8 @@
     for d in range(1, lines):
         forward_line(d)
         forward_pair(d - 1)
+        if d == 1:
+            lend()
     bridge = jnp.logical_or(z == 1, z == lines - 2)
     keep = jnp.where(z == 1, lines - 1, 0) * X + (1 - x)
     keep = jnp.where(bridge, keep, me)
@@ -276,10 +317,19 @@
     late_z[...] = place(keep, LATE_PAIR)[...]
     forward_pair(lines - 1)
 
+    arrive(DOWN, mate * X + 1 - x, LATE_LINE, inner, True)
     for t in range(len(outs)):
-        skipped = LATE_LINE[2] * (t == LATE_LINE[0])
-        collect(t, lines * units_of(LINE, t) - skipped)
-        drain(SIDE, t, lines * units_of(LINE, t) + units_of(PAIR, t) - skipped)
+        if t != LATE_LINE[0]:
+            collect(t, lines * units_of(LINE, t))
+            drain(SIDE, t, lines * units_of(LINE, t) + units_of(PAIR, t))
+            continue
+        for cond, skipped in ((inner, 2 * LATE_LINE[2]), (jnp.logical_not(inner), LATE_LINE[2])):
+
+            @pl.when(cond)
+            def _(t=t, skipped=skipped):
+                units = lines * units_of(LINE, t)
+                collect(t, units - skipped - LATE_LINE[2])
+                drain(SIDE, t, units + units_of(PAIR, t) - skipped)
     norm_side(me).wait_send()
     if widths > 1:
         tiles().wait_send()
@@ -292,7 +342,9 @@
                 feeder = k == (lines - 2 if way == UP else 1)
                 for t in range(len(outs)):
                     skipped = LATE_PAIR[2] * (feeder and t == LATE_PAIR[0])
-                    drain(way, t, planes * (units_of(LINE, t) + X * units_of(PAIR, t)) - skipped)
+                    lent = (k >= 2 and k - 1 < lines // 2) if way == DOWN else (k + 1 >= lines // 2 and k + 2 < lines)
+                    lent = LATE_LINE[2] * (lent and t == LATE_LINE[0])
+                    drain(way, t, planes * (units_of(LINE, t) + X * units_of(PAIR, t)) - skipped + lent)
                 norm_copy(0, planes * plane_rows, way, 0, (partner, w)).wait_send()
 
 
@@ -324,12 +376,14 @@
             flip(low_gate), flip(low_up), flip(high_down),
             pltpu.SemaphoreType.DMA((WAYS * 3,)),
             pltpu.SemaphoreType.DMA((lines * len(LINE),)),
-            pltpu.SemaphoreType.DMA((shards * len(PAIR),)),
+            pltpu.SemaphoreType.DMA((lines * 3,)),
             pltpu.SemaphoreType.DMA((3,)),
             pltpu.SemaphoreType.DMA((4,)),
             pltpu.SemaphoreType.DMA((2 + lines,)),
             pltpu.SemaphoreType.DMA((4,)),
             pltpu.SemaphoreType.DMA((8,)),
+            pltpu.SemaphoreType.DMA((2,)),
+            pltpu.SemaphoreType.REGULAR((3,)),
         ],
         compiler_params=pltpu.CompilerParams(collective_id=0, has_side_effects=True, vmem_limit_bytes=16 * 2**20),
     )(*(pltpu.with_memory_space_constraint(a, pltpu.HBM) for a in args))
@@ -374,7 +428,7 @@
     )(gate, up, down, rows)
 
 
-def late_kernel(lines, up, down, late_x, late_z, o_up, o_down, v_x, v_z, sem):
+def late_kernel(lines, up, down, late_z, late_x, o_up, o_down, sem):
     me = lax.axis_index("shard")
     z, x = me // X, me % X
     wide, tall = late_z.shape[1], up.shape[0]
@@ -383,39 +437,26 @@
     block = (far_plane(z, lines) * X + (1 - x)) * wide
     block = pl.ds(pl.multiple_of(block, wide), wide)
     inner = lambda c: pl.ds(c[1] * unit, c[2] * unit)
-    get_x = pltpu.make_async_copy(late_x, v_x, sem.at[0])
-    get_z = pltpu.make_async_copy(late_z, v_z, sem.at[1])
-    put_x = pltpu.make_async_copy(v_x, o_down.at[block, inner(LATE_LINE)], sem.at[2])
-    put_z = pltpu.make_async_copy(v_z, o_up.at[inner(LATE_PAIR), block], sem.at[3])
-    get_x.start()
-    pl.when(end)(get_z.start)
-    get_x.wait()
+    put_x = pltpu.make_async_copy(late_x, o_down.at[block, inner(LATE_LINE)], sem.at[0])
+    put_z = pltpu.make_async_copy(late_z, o_up.at[inner(LATE_PAIR), block], sem.at[1])
     put_x.start()
-
-    @pl.when(end)
-    def _():
-        get_z.wait()
-        put_z.start()
-        put_z.wait()
-
+    pl.when(end)(put_z.start)
     put_x.wait()
+    pl.when(end)(put_z.wait)
 
 
 def write_late(lines, up, down, late_x, late_z):
     any_ = pl.BlockSpec(memory_space=pl.ANY)
+    vmem = pl.BlockSpec(memory_space=pltpu.VMEM)
     return pl.pallas_call(
         functools.partial(late_kernel, lines),
         out_shape=tuple(jax.ShapeDtypeStruct(a.shape, a.dtype) for a in (up, down)),
-        in_specs=[any_] * 4,
+        in_specs=[any_] * 2 + [vmem] * 2,
         out_specs=(any_,) * 2,
         input_output_aliases={0: 0, 1: 1},
-        scratch_shapes=[
-            pltpu.VMEM(late_x.shape, late_x.dtype),
-            pltpu.VMEM(late_z.shape, late_z.dtype),
-            pltpu.SemaphoreType.DMA((4,)),
-        ],
+        scratch_shapes=[pltpu.SemaphoreType.DMA((2,))],
         compiler_params=pltpu.CompilerParams(vmem_limit_bytes=4 * 2**20),
-    )(up, down, late_x, late_z)
+    )(up, down, late_z, late_x)
 
 
 def body(
@@ -453,8 +494,8 @@
     )
     gate, up, down, rows, late_x, late_z = gather_all(shards, widths, args)
     per = LANES // count
+    late_z = lax.ppermute(late_z, "shard", [(s, s ^ X) for s in range(shards)])
     late_x = lax.ppermute(late_x, "shard", [(s, s ^ 1) for s in range(shards)])
-    late_z = lax.ppermute(late_z, "shard", [(s, s ^ X) for s in range(shards)])
     gate, up, down, norm = write_out(gate, up, down, rows.reshape(-1, per, LANES))
     up, down = write_late(shards // X, up, down, late_x, late_z)
     return gate, up, down, norm.reshape(-1)

time: 248 us -> 246 us (level)
  transfers between devices with their start and end apart: 2 -> 2, of which waited for: 0 -> 2; matrix products, arithmetic and copies ran while one was open for 0% -> 0% of each run, Pallas kernels for 3% -> 3%
where the time goes in v4:
time: 246 us
  Pallas kernels  243 us (99%)
    pallas_call x1, Pallas kernels, gather_all(): pl.pallas_call(functools.partial(gather_kernel, shards, widths), out_shap...  234 us
    pallas_call x1, Pallas kernels, write_out(): pl.pallas_call(write_kernel, out_shape=tuple((jax.ShapeDtypeStruct(a.shap...  8.49 us
  transfers between devices with their start and end apart: 2, of which 2 were waited for; matrix products, arithmetic and copies ran while one was open for 0% of the time, Pallas kernels for 3%

profile of v4, /device:TPU:0, one launch (start us, length us, event | category | flops | bytes accessed | tf_op | source)
XLA Modules:
  0.0 245.6 jit_solution(9041964615836471226)
XLA Ops:
  0.6 233.9 %shard_map.138 = (bf16[2048,2048]{1,0:T(8,128)(2,1)S(1)}, bf16[2048,2048]{1,0:T(8,128)(2,1)S(1)}, bf16[2048,2048]{1,0:T(8,128)(2,1)S(1)}, f32[32,1,128]{2,1,0:T(...) custom-call(bf16[256,2048]{1,0:T(8,128)(2,1)} %w_gate.1, bf16[64,256]{1,0:T(8,128)(2,1)} %bitcast.9, ...), custom_call_target="tpu_custom_call" | custom-call | tf_op jit(solution)/shard_map/pallas_call | solution.py:360
  234.6 0.1 collective-permute-start
  234.6 1.3 collective-permute-start.1
  235.9 8.5 %shard_map.139 = (bf16[2048,2048]{1,0:T(8,128)(2,1)}, bf16[2048,2048]{1,0:T(8,128)(2,1)}, bf16[2048,2048]{1,0:T(8,128)(2,1)}, bf16[16,128]{1,0:T(8,128)(2,1)}) custom-call(bf16[2048,2048]{1,0:T(8,128)(2,1)S(1)} %get-tuple-element.16.gate, bf16[2048,2048]{1,0:T(8,128)(2,1)S(1)} %get-tuple-element.17.up, bf16[2048,2048]{1,0:T(8,128)(2,1)S(1)} %get-tuple-element.18.down, ...), custom_call_target="tpu_custom_call" | custom-call | flops 2000000000 | bytes 50331648 | tf_op jit(solution)/shard_map/pallas_call | solution.py:419
  244.4 0.2 collective-permute-done.late_z
  244.6 0.1 collective-permute-done.1.late_x
  244.7 0.9 shard_map.140
Async XLA Ops:
  234.6 10.1 %collective-permute-start = (bf16[768,256]{1,0:T(8,128)(2,1)S(1)}, bf16[768,256]{1,0:T(8,128)(2,1)S(1)}, u32[]{:S(2)}, u32[]{:S(2)}) collective-permute-start(bf16[768,256]{1,0:T(8,128)(2,1)S(1)} %get-tuple-element.23), channel_id=1, source_target_pairs={{0,8},{4,12},{8,0},{12,4},{16,24},{20,28},{24,16},{28,20},{1,9},{5... | collective-permute-start | bytes 1179656 | tf_op jit(solution)/shard_map/ppermute | solution.py:497
  234.6 10.1 %collective-permute-start.1 = (bf16[256,768]{1,0:T(8,128)(2,1)S(1)}, bf16[256,768]{1,0:T(8,128)(2,1)S(1)}, u32[]{:S(2)}, u32[]{:S(2)}) collective-permute-start(bf16[256,768]{1,0:T(8,128)(2,1)S(1)} %get-tuple-element.24), channel_id=1, source_target_pairs={{0,4},{4,0},{8,12},{12,8},{16,20},{20,16},{24,28},{28,24},{1,5},{5... | collective-permute-start | bytes 1179656 | tf_op jit(solution)/shard_map/ppermute | solution.py:498

commit v5 on v4

--- a/solution.py
+++ b/solution.py
@@ -1,4 +1,5 @@
 import functools
+import math
 
 import jax
 import jax.numpy as jnp
@@ -16,6 +17,7 @@
 LINE = ((0, 0, 16), (1, 0, 8), (2, 0, 10), (2, 10, 6))
 PAIR = ((1, 8, 2), (1, 10, 6))
 WHOLE = (1, 8, 8)
+BUNDLES = (LINE[:1], LINE[1:3], LINE[3:])
 LATE_LINE, LATE_PAIR = LINE[-1], PAIR[-1]
 ORDER = (
     ((0, 0, 1), LINE[0]), ((0, 1, 3), LINE[0]), ((0, 4, 12), LINE[0]),
@@ -29,8 +31,11 @@
 WRITE_FLOPS = 2 * 10**9
 
 
-def units_of(pieces, t):
-    return sum(n for array, _, n in pieces if array == t)
+def units_of(pieces, arrays=(0, 1, 2)):
+    return sum(n for array, _, n in pieces if array in arrays)
+
+
+SHARES = ((0, 1), (2,))
 
 
 def merged(w, low, high):
@@ -65,7 +70,7 @@
     o_gate, o_up, o_down, o_norm, late_x, late_z,
     v_gate, v_up, v_down, v_low_gate, v_low_up, v_low_down, v_high_gate, v_high_up, v_high_down,
     v_train, v_step, l_gate, l_up, h_down,
-    send_sem, line_sem, pair_sem, side_sem, norm_send, norm_recv, load_sem, small_sem, extra_sem, ready,
+    send_sem, line_sem, pair_sem, side_sem, extra_sem, norm_send, norm_recv, load_sem, ready,
 ):
     lines = shards // X
     me, w = lax.axis_index("shard"), lax.axis_index("width")
@@ -76,21 +81,31 @@
     unit = tall // UNITS
 
     head = ORDER[0][0][2] * unit
-    loads = [
-        pltpu.make_async_copy(w_gate.at[:, pl.ds(0, head)], v_gate.at[:, pl.ds(0, head)], load_sem.at[0]),
-        pltpu.make_async_copy(w_gate.at[:, pl.ds(head, tall - head)], v_gate.at[:, pl.ds(head, tall - head)], load_sem.at[1]),
-        pltpu.make_async_copy(w_up, v_up, load_sem.at[2]),
-        pltpu.make_async_copy(w_down, v_down, load_sem.at[3]),
-    ]
-    smalls = (
-        (low_gate, v_low_gate), (high_gate, v_high_gate),
-        (low_up, v_low_up), (high_up, v_high_up),
-        (low_down, v_low_down), (high_down, v_high_down),
-        (train, v_train), (step, v_step),
+    loads = (
+        (
+            (low_gate, v_low_gate),
+            (high_gate, v_high_gate),
+            (w_gate.at[:, pl.ds(0, head)], v_gate.at[:, pl.ds(0, head)]),
+        ),
+        ((w_gate.at[:, pl.ds(head, tall - head)], v_gate.at[:, pl.ds(head, tall - head)]),),
+        ((low_up, v_low_up), (high_up, v_high_up), (w_up, v_up)),
+        ((low_down, v_low_down), (high_down, v_high_down), (w_down, v_down)),
+        ((train, v_train),),
+        ((step, v_step),),
     )
-    small = [pltpu.make_async_copy(a, b, small_sem.at[i]) for i, (a, b) in enumerate(smalls)]
-    for copy in small[:2] + loads[:2] + small[2:4] + loads[2:3] + small[4:6] + loads[3:] + small[6:]:
-        copy.start()
+    for i, pairs in enumerate(loads):
+        for src, dst in pairs:
+            pltpu.make_async_copy(src, dst, load_sem.at[i]).start()
+
+    def bulk(elements):
+        return o_gate.at[pl.ds(0, elements // o_gate.shape[1])]
+
+    def loaded(i):
+        if len(loads[i]) == 1:
+            pltpu.make_async_copy(*loads[i][0], load_sem.at[i]).wait()
+        else:
+            ref = bulk(sum(math.prod(dst.shape) for _, dst in loads[i]))
+            pltpu.make_async_copy(ref, ref, load_sem.at[i]).wait()
 
     def target(way):
         return {UP: me + X, DOWN: me - X, SIDE: partner}[way]
@@ -124,21 +139,26 @@
         inner = pl.ds(first * unit, n * unit)
         return outs[t].at[inner, block] if t < 2 else outs[t].at[block, inner]
 
-    def receipt(way, s, whole, extra):
-        if whole == WHOLE:
-            return pair_sem.at[s // X * 3]
-        if whole in PAIR:
-            return pair_sem.at[s // X * 3 + 1 + PAIR.index(whole)]
+    def share(t):
+        return 0 if t in SHARES[0] else 1
+
+    def receipt(way, plane, whole, extra):
         if extra:
             return extra_sem.at[0 if way == SIDE else 1]
-        return side_sem.at[whole[0]] if way == SIDE else line_sem.at[s // X * len(LINE) + LINE.index(whole)]
+        if way == SIDE:
+            return extra_sem.at[2 + PAIR.index(whole)] if whole in PAIR else side_sem.at[share(whole[0])]
+        slot = plane if way == UP else plane - 1
+        for i, bundle in enumerate(BUNDLES):
+            if whole in bundle:
+                return line_sem.at[slot * len(BUNDLES) + i]
+        return pair_sem.at[slot * 2 + (1 if whole == LATE_PAIR else 0)]
 
     def remote(way, s, c, whole, extra=False):
         return pltpu.make_async_remote_copy(
             src_ref=place(s, c),
             dst_ref=place(s, c),
-            send_sem=send_sem.at[way * len(outs) + c[0]],
-            recv_sem=receipt(way, s, whole, extra),
+            send_sem=send_sem.at[way * len(SHARES) + share(c[0])],
+            recv_sem=receipt(way, s // X, whole, extra),
             device_id=(target(way), w),
             device_id_type=MESH,
         )
@@ -146,44 +166,37 @@
     def send(way, s, c, cond=None, whole=None, extra=False):
         when(both(cond, has(way)), lambda: remote(way, s, c, whole or c, extra).start())
 
-    def arrive(way, s, c, cond=None, extra=False):
-        when(cond, lambda: remote(way, s, c, c, extra).wait_recv())
-
-    def bulk(t, elements):
-        return outs[t].at[pl.ds(0, elements // outs[t].shape[1])]
-
-    def drain(way, t, units):
-        ref = bulk(t, units * unit * wide)
-        pltpu.make_async_remote_copy(
-            src_ref=ref, dst_ref=ref, send_sem=send_sem.at[way * len(outs) + t], recv_sem=side_sem.at[t],
-            device_id=(partner, w), device_id_type=MESH,
-        ).wait_send()
-
-    def collect(t, units):
-        ref = bulk(t, units * unit * wide)
-        pltpu.make_async_remote_copy(
-            src_ref=ref, dst_ref=ref, send_sem=send_sem.at[t], recv_sem=side_sem.at[t],
-            device_id=(partner, w), device_id_type=MESH,
-        ).wait_recv()
-
-    waits = {ORDER[0][0]: loads[:1], ORDER[1][0]: loads[1:2]}
+    def bytes_of(units, send, recv):
+        ref = bulk(units * unit * wide)
+        return pltpu.make_async_remote_copy(
+            src_ref=ref, dst_ref=ref, send_sem=send, recv_sem=recv, device_id=(partner, w), device_id_type=MESH
+        )
+
+    def arrive(way, plane, pieces, cond=None, extra=False):
+        sem = receipt(way, plane, pieces[0], extra)
+        when(cond, lambda: bytes_of(units_of(pieces), send_sem.at[0], sem).wait_recv())
+
+    def drain(way, i, units):
+        bytes_of(units, send_sem.at[way * len(SHARES) + i], side_sem.at[i]).wait_send()
+
+    def collect(i, units):
+        bytes_of(units, send_sem.at[i], side_sem.at[i]).wait_recv()
+
     seen = set()
 
     def compute(c):
         t, first, n = c
-        pending = waits.get(c, [])
         if t not in seen:
             seen.add(t)
-            pending = small[2 * t : 2 * t + 2] + (pending if t == 0 else loads[t + 1 : t + 2])
-        for copy in pending:
-            copy.wait()
-        if len(pending) > 1:
+            loaded((0, 2, 3)[t])
             if t == 0:
                 l_gate[...] = v_low_gate[...].T
             elif t == 1:
                 l_up[...] = v_low_up[...].T
             else:
                 h_down[...] = v_high_down[...].T
+        elif c == ORDER[1][0]:
+            loaded(1)
         columns = pl.ds(pl.multiple_of(me * wide, wide), wide)
 
         @pl.loop(0, n * unit // LANES)
@@ -199,10 +212,9 @@
         if whole in LINE:
             send(UP, me, c, None, whole)
 
+    enter()
     for k, (c, whole) in enumerate(ORDER):
         compute(c)
-        if k == 0:
-            enter()
         if k == 1:
             when(has(UP), lambda: pl.semaphore_wait(ready.at[UP], 1))
             send_up(*ORDER[0])
@@ -224,8 +236,8 @@
             device_id=dev, device_id_type=MESH,
         )
 
-    for copy in small[6:]:
-        copy.wait()
+    loaded(4)
+    loaded(5)
     gain = v_train[...] + v_step[...]
     row = jnp.concatenate([gain] * (LANES // gain.shape[1]), axis=1)
     o_norm[pl.ds(me * widths + w, 1)] = row.reshape(1, 1, LANES)
@@ -235,7 +247,9 @@
     tiles = lambda: norm_copy(0, widths - 1, 3, 0, (partner, w))
     norm_side = lambda s: norm_copy(s * widths, widths, SIDE, 1, (partner, w))
     plane_rows = X * widths
-    norm_plane = lambda way, plane: norm_copy(plane * plane_rows, plane_rows, way, 2 + plane, (target(way), w))
+    norm_plane = lambda way, plane: norm_copy(
+        plane * plane_rows, plane_rows, way, 2 + (plane if way == UP else plane - 1), (target(way), w)
+    )
     if widths > 1:
         tiles().wait_recv()
     norm_side(me).start()
@@ -253,7 +267,7 @@
         return jnp.logical_and(plane != far, jnp.logical_not(jnp.logical_and(inner, plane == mate)))
 
     def lend():
-        arrive(SIDE, partner, LATE_LINE, None, True)
+        arrive(SIDE, z, (LATE_LINE,), None, True)
         for way in (UP, DOWN):
             send(way, partner, LATE_LINE, lends[way], None, True)
 
@@ -261,12 +275,12 @@
         return ((UP, z - d, z >= d), (DOWN, z + d, z + d < lines))
 
     def forward_line(d):
-        for c in LINE:
+        for pieces in BUNDLES:
             for way, plane, cond in hops(d):
-                s = plane * X + x
-                arrive(way, s, c, cond)
-                send(way, s, c, cond)
-                send(SIDE, s, c, both(cond, by_side(plane)) if c == LATE_LINE else cond)
+                arrive(way, plane, pieces, cond)
+                for c in pieces:
+                    send(way, plane * X + x, c, cond)
+                    send(SIDE, plane * X + x, c, both(cond, by_side(plane)) if c == LATE_LINE else cond)
 
     source = {UP: 0, DOWN: lines - 1}
     feeds = {UP: z == lines - 2, DOWN: z == 1}
@@ -277,12 +291,12 @@
             cond = both(cond, jnp.logical_not(late))
         send(way, plane * X + (x + j) % X, c, cond)
 
-    def arrive_pair(way, plane, j, c, cond):
-        if c == LATE_PAIR:
+    def arrive_pair(way, plane, pieces, cond):
+        if LATE_PAIR in pieces:
             end = {UP: z == lines - 1, DOWN: z == 0}[way]
             late = jnp.logical_and(end, plane == source[way])
             cond = both(cond, jnp.logical_not(late))
-        arrive(way, plane * X + (x + j) % X, c, cond)
+        arrive(way, plane, pieces, cond)
 
     def forward_pair(d):
         if d == 0:
@@ -292,17 +306,17 @@
             for way in (UP, DOWN):
                 when(has(way), lambda way=way: norm_plane(way, z).start())
             for c in PAIR:
-                arrive(SIDE, partner, c)
+                arrive(SIDE, z, (c,))
                 send_pair(UP, z, 1, c)
                 send_pair(DOWN, z, 1, c)
             return
         for way, plane, cond in hops(d):
             when(cond, lambda way=way, plane=plane: norm_plane(way, plane).wait_recv())
             when(both(cond, has(way)), lambda way=way, plane=plane: norm_plane(way, plane).start())
-        for j, pieces in enumerate(((WHOLE,), PAIR)):
-            for c in pieces:
-                for way, plane, cond in hops(d):
-                    arrive_pair(way, plane, j, c, cond)
+        for bundle in (((WHOLE, 0), (PAIR[0], 1)), ((LATE_PAIR, 1),)):
+            for way, plane, cond in hops(d):
+                arrive_pair(way, plane, [c for c, _ in bundle], cond)
+                for c, j in bundle:
                     send_pair(way, plane, j, c, cond)
 
     for d in range(1, lines):
@@ -317,34 +331,39 @@
     late_z[...] = place(keep, LATE_PAIR)[...]
     forward_pair(lines - 1)
 
-    arrive(DOWN, mate * X + 1 - x, LATE_LINE, inner, True)
-    for t in range(len(outs)):
-        if t != LATE_LINE[0]:
-            collect(t, lines * units_of(LINE, t))
-            drain(SIDE, t, lines * units_of(LINE, t) + units_of(PAIR, t))
+    arrive(DOWN, mate, (LATE_LINE,), inner, True)
+    lent = share(LATE_LINE[0])
+    for i, arrays in enumerate(SHARES):
+        units = lines * units_of(LINE, arrays)
+        own = units_of(PAIR, arrays)
+        if i != lent:
+            collect(i, units)
+            drain(SIDE, i, units + own)
             continue
         for cond, skipped in ((inner, 2 * LATE_LINE[2]), (jnp.logical_not(inner), LATE_LINE[2])):
 
             @pl.when(cond)
-            def _(t=t, skipped=skipped):
-                units = lines * units_of(LINE, t)
-                collect(t, units - skipped - LATE_LINE[2])
-                drain(SIDE, t, units + units_of(PAIR, t) - skipped)
+            def _(i=i, units=units - skipped, own=own):
+                collect(i, units - LATE_LINE[2])
+                drain(SIDE, i, units + own)
     norm_side(me).wait_send()
     if widths > 1:
         tiles().wait_send()
     for way in (UP, DOWN):
         for k in range(lines):
             planes = k + 1 if way == UP else lines - k
+            if planes == lines:
+                continue
 
             @pl.when(both(z == k, has(way)))
             def _(way=way, planes=planes):
                 feeder = k == (lines - 2 if way == UP else 1)
-                for t in range(len(outs)):
-                    skipped = LATE_PAIR[2] * (feeder and t == LATE_PAIR[0])
-                    lent = (k >= 2 and k - 1 < lines // 2) if way == DOWN else (k + 1 >= lines // 2 and k + 2 < lines)
-                    lent = LATE_LINE[2] * (lent and t == LATE_LINE[0])
-                    drain(way, t, planes * (units_of(LINE, t) + X * units_of(PAIR, t)) - skipped + lent)
+                lends_here = (k >= 2 and k - 1 < lines // 2) if way == DOWN else (k + 1 >= lines // 2 and k + 2 < lines)
+                for i, arrays in enumerate(SHARES):
+                    units = planes * (units_of(LINE, arrays) + X * units_of(PAIR, arrays))
+                    units -= LATE_PAIR[2] * (feeder and i == share(LATE_PAIR[0]))
+                    units += LATE_LINE[2] * (lends_here and i == lent)
+                    drain(way, i, units)
                 norm_copy(0, planes * plane_rows, way, 0, (partner, w)).wait_send()
 
 
@@ -374,15 +393,14 @@
             like(high_gate), like(high_up), like(high_down),
             like(train), like(step),
             flip(low_gate), flip(low_up), flip(high_down),
-            pltpu.SemaphoreType.DMA((WAYS * 3,)),
-            pltpu.SemaphoreType.DMA((lines * len(LINE),)),
-            pltpu.SemaphoreType.DMA((lines * 3,)),
-            pltpu.SemaphoreType.DMA((3,)),
+            pltpu.SemaphoreType.DMA((WAYS * len(SHARES),)),
+            pltpu.SemaphoreType.DMA(((lines - 1) * len(BUNDLES),)),
+            pltpu.SemaphoreType.DMA(((lines - 1) * 2,)),
+            pltpu.SemaphoreType.DMA((len(SHARES),)),
+            pltpu.SemaphoreType.DMA((2 + len(PAIR),)),
             pltpu.SemaphoreType.DMA((4,)),
-            pltpu.SemaphoreType.DMA((2 + lines,)),
-            pltpu.SemaphoreType.DMA((4,)),
-            pltpu.SemaphoreType.DMA((8,)),
-            pltpu.SemaphoreType.DMA((2,)),
+            pltpu.SemaphoreType.DMA((1 + lines,)),
+            pltpu.SemaphoreType.DMA((6,)),
             pltpu.SemaphoreType.REGULAR((3,)),
         ],
         compiler_params=pltpu.CompilerParams(collective_id=0, has_side_effects=True, vmem_limit_bytes=16 * 2**20),
@@ -393,7 +411,7 @@
     pairs = ((gate, o_gate), (up, o_up), (down, o_down))
     part = gate.shape[0] // WRITES
     copies = [
-        pltpu.make_async_copy(a.at[pl.ds(j * part, part)], b.at[pl.ds(j * part, part)], sem.at[i * WRITES + j])
+        pltpu.make_async_copy(a.at[pl.ds(j * part, part)], b.at[pl.ds(j * part, part)], sem.at[i])
         for i, (a, b) in enumerate(pairs)
         for j in range(WRITES)
     ]
@@ -405,10 +423,10 @@
     for j in range(1, per):
         line = jnp.where(lane == j, rows[:, j, :], line)
     norm[...] = line.astype(norm.dtype)
-    last = pltpu.make_async_copy(norm, o_norm, sem.at[len(copies)])
+    last = pltpu.make_async_copy(norm, o_norm, sem.at[len(pairs)])
     last.start()
-    for copy in copies:
-        copy.wait()
+    for i, (a, b) in enumerate(pairs):
+        pltpu.make_async_copy(a, b, sem.at[i]).wait()
     last.wait()
 
 
@@ -422,7 +440,7 @@
         + (jax.ShapeDtypeStruct(norm, jnp.bfloat16),),
         in_specs=[any_] * 3 + [vmem],
         out_specs=(any_,) * 4,
-        scratch_shapes=[pltpu.VMEM(norm, jnp.bfloat16), pltpu.SemaphoreType.DMA((3 * WRITES + 1,))],
+        scratch_shapes=[pltpu.VMEM(norm, jnp.bfloat16), pltpu.SemaphoreType.DMA((4,))],
         cost_estimate=pl.CostEstimate(flops=WRITE_FLOPS, bytes_accessed=2 * 3 * gate.size * 2, transcendentals=0),
         compiler_params=pltpu.CompilerParams(vmem_limit_bytes=4 * 2**20),
     )(gate, up, down, rows)
@@ -476,7 +494,7 @@
 ):
     count = norm_train.shape[0]
     wide, tall = w_gate.shape
-    if shards % (2 * X) or wide % LANES or tall % (UNITS * LANES) or LANES % count or (shards * widths * count) % LANES:
+    if shards % (2 * X) or shards > 4 * X or wide % LANES or tall % (UNITS * LANES) or LANES % count or (shards * widths * count) % LANES:
         gate = merged(w_gate, low_gate, high_gate)
         up = merged(w_up, low_up, high_up)
         down = merged(w_down, low_down, high_down)

time: 246 us -> 246 us (level)
  no operation moved by 1% of the time
where the time goes in v5:
time: 246 us; the launch traced here: 245 us
  Pallas kernels  243 us (99%)
    pallas_call x1, Pallas kernels, gather_all(): pl.pallas_call(functools.partial(gather_kernel, shards, widths), out_shap...  233 us
    pallas_call x1, Pallas kernels, write_out(): pl.pallas_call(write_kernel, out_shape=tuple((jax.ShapeDtypeStruct(a.shap...  8.41 us
  transfers between devices with their start and end apart: 2, of which 2 were waited for; matrix products, arithmetic and copies ran while one was open for 0% of the time, Pallas kernels for 3%

profile of v5, /device:TPU:0, one launch (start us, length us, event | category | flops | bytes accessed | tf_op | source)
XLA Modules:
  0.0 245.4 jit_solution(453593097502398906)
XLA Ops:
  0.6 233.4 %shard_map.138 = (bf16[2048,2048]{1,0:T(8,128)(2,1)S(1)}, bf16[2048,2048]{1,0:T(8,128)(2,1)S(1)}, bf16[2048,2048]{1,0:T(8,128)(2,1)S(1)}, f32[32,1,128]{2,1,0:T(...) custom-call(bf16[256,2048]{1,0:T(8,128)(2,1)} %w_gate.1, bf16[64,256]{1,0:T(8,128)(2,1)} %bitcast.9, ...), custom_call_target="tpu_custom_call" | custom-call | tf_op jit(solution)/shard_map/pallas_call | solution.py:379
  234.0 0.1 collective-permute-start
  234.1 1.5 collective-permute-start.1
  235.6 8.4 %shard_map.139 = (bf16[2048,2048]{1,0:T(8,128)(2,1)}, bf16[2048,2048]{1,0:T(8,128)(2,1)}, bf16[2048,2048]{1,0:T(8,128)(2,1)}, bf16[16,128]{1,0:T(8,128)(2,1)}) custom-call(bf16[2048,2048]{1,0:T(8,128)(2,1)S(1)} %get-tuple-element.16.gate, bf16[2048,2048]{1,0:T(8,128)(2,1)S(1)} %get-tuple-element.17.up, bf16[2048,2048]{1,0:T(8,128)(2,1)S(1)} %get-tuple-element.18.down, ...), custom_call_target="tpu_custom_call" | custom-call | flops 2000000000 | bytes 50331648 | tf_op jit(solution)/shard_map/pallas_call | solution.py:437
  244.0 0.5 collective-permute-done.late_z
  244.4 0.1 collective-permute-done.1.late_x
  244.5 0.9 shard_map.140
Async XLA Ops:
  234.0 10.4 %collective-permute-start = (bf16[768,256]{1,0:T(8,128)(2,1)S(1)}, bf16[768,256]{1,0:T(8,128)(2,1)S(1)}, u32[]{:S(2)}, u32[]{:S(2)}) collective-permute-start(bf16[768,256]{1,0:T(8,128)(2,1)S(1)} %get-tuple-element.23), channel_id=1, source_target_pairs={{0,8},{4,12},{8,0},{12,4},{16,24},{20,28},{24,16},{28,20},{1,9},{5... | collective-permute-start | bytes 1179656 | tf_op jit(solution)/shard_map/ppermute | solution.py:515
  234.1 10.4 %collective-permute-start.1 = (bf16[256,768]{1,0:T(8,128)(2,1)S(1)}, bf16[256,768]{1,0:T(8,128)(2,1)S(1)}, u32[]{:S(2)}, u32[]{:S(2)}) collective-permute-start(bf16[256,768]{1,0:T(8,128)(2,1)S(1)} %get-tuple-element.24), channel_id=1, source_target_pairs={{0,4},{4,0},{8,12},{12,8},{16,20},{20,16},{24,28},{28,24},{1,5},{5... | collective-permute-start | bytes 1179656 | tf_op jit(solution)/shard_map/ppermute | solution.py:516

commit v6 on v5

--- a/solution.py
+++ b/solution.py
@@ -212,9 +212,10 @@
         if whole in LINE:
             send(UP, me, c, None, whole)
 
-    enter()
     for k, (c, whole) in enumerate(ORDER):
         compute(c)
+        if k == 0:
+            enter()
         if k == 1:
             when(has(UP), lambda: pl.semaphore_wait(ready.at[UP], 1))
             send_up(*ORDER[0])

time: 246 us -> 245 us (level)
  no operation moved by 1% of the time
where the time goes in v6:
time: 245 us
  Pallas kernels  243 us (99%)
    pallas_call x1, Pallas kernels, gather_all(): pl.pallas_call(functools.partial(gather_kernel, shards, widths), out_shap...  234 us
    pallas_call x1, Pallas kernels, write_out(): pl.pallas_call(write_kernel, out_shape=tuple((jax.ShapeDtypeStruct(a.shap...  8.41 us
  transfers between devices with their start and end apart: 2, of which 2 were waited for; matrix products, arithmetic and copies ran while one was open for 0% of the time, Pallas kernels for 3%

profile of v6, /device:TPU:0, one launch (start us, length us, event | category | flops | bytes accessed | tf_op | source)
XLA Modules:
  0.0 245.3 jit_solution(10397127036427168339)
XLA Ops:
  0.6 233.6 %shard_map.138 = (bf16[2048,2048]{1,0:T(8,128)(2,1)S(1)}, bf16[2048,2048]{1,0:T(8,128)(2,1)S(1)}, bf16[2048,2048]{1,0:T(8,128)(2,1)S(1)}, f32[32,1,128]{2,1,0:T(...) custom-call(bf16[256,2048]{1,0:T(8,128)(2,1)} %w_gate.1, bf16[64,256]{1,0:T(8,128)(2,1)} %bitcast.9, ...), custom_call_target="tpu_custom_call" | custom-call | tf_op jit(solution)/shard_map/pallas_call | solution.py:380
  234.3 0.1 collective-permute-start
  234.4 1.3 collective-permute-start.1
  235.7 8.4 %shard_map.139 = (bf16[2048,2048]{1,0:T(8,128)(2,1)}, bf16[2048,2048]{1,0:T(8,128)(2,1)}, bf16[2048,2048]{1,0:T(8,128)(2,1)}, bf16[16,128]{1,0:T(8,128)(2,1)}) custom-call(bf16[2048,2048]{1,0:T(8,128)(2,1)S(1)} %get-tuple-element.16.gate, bf16[2048,2048]{1,0:T(8,128)(2,1)S(1)} %get-tuple-element.17.up, bf16[2048,2048]{1,0:T(8,128)(2,1)S(1)} %get-tuple-element.18.down, ...), custom_call_target="tpu_custom_call" | custom-call | flops 2000000000 | bytes 50331648 | tf_op jit(solution)/shard_map/pallas_call | solution.py:438
  244.1 0.2 collective-permute-done.late_z
  244.3 0.1 collective-permute-done.1.late_x
  244.4 0.9 shard_map.140
Async XLA Ops:
  234.3 10.1 %collective-permute-start = (bf16[768,256]{1,0:T(8,128)(2,1)S(1)}, bf16[768,256]{1,0:T(8,128)(2,1)S(1)}, u32[]{:S(2)}, u32[]{:S(2)}) collective-permute-start(bf16[768,256]{1,0:T(8,128)(2,1)S(1)} %get-tuple-element.23), channel_id=1, source_target_pairs={{0,8},{4,12},{8,0},{12,4},{16,24},{20,28},{24,16},{28,20},{1,9},{5... | collective-permute-start | bytes 1179656 | tf_op jit(solution)/shard_map/ppermute | solution.py:516
  234.4 10.1 %collective-permute-start.1 = (bf16[256,768]{1,0:T(8,128)(2,1)S(1)}, bf16[256,768]{1,0:T(8,128)(2,1)S(1)}, u32[]{:S(2)}, u32[]{:S(2)}) collective-permute-start(bf16[256,768]{1,0:T(8,128)(2,1)S(1)} %get-tuple-element.24), channel_id=1, source_target_pairs={{0,4},{4,0},{8,12},{12,8},{16,20},{20,16},{24,28},{28,24},{1,5},{5... | collective-permute-start | bytes 1179656 | tf_op jit(solution)/shard_map/ppermute | solution.py:517

commit v7 on v6

--- a/solution.py
+++ b/solution.py
@@ -208,24 +208,19 @@
             else:
                 o_down[columns, at] = merged(v_down[at, :].T, h_down[...], v_low_down[:, at])
 
-    def send_up(c, whole):
-        if whole in LINE:
-            send(UP, me, c, None, whole)
-
     for k, (c, whole) in enumerate(ORDER):
         compute(c)
         if k == 0:
             enter()
-        if k == 1:
-            when(has(UP), lambda: pl.semaphore_wait(ready.at[UP], 1))
-            send_up(*ORDER[0])
         if whole in LINE:
             send(DOWN, me, c, None, whole)
         if k == 0:
             pl.when(x == 0)(lambda: pl.semaphore_wait(ready.at[SIDE], 1))
-        else:
-            send_up(c, whole)
         send(SIDE, me, c, None, whole, c == LATE_LINE)
+        if k == 0:
+            when(has(UP), lambda: pl.semaphore_wait(ready.at[UP], 1))
+        if whole in LINE:
+            send(UP, me, c, None, whole)
 
     def norm_rows(begin, count):
         return o_norm.at[pl.ds(begin, count)]

time: 245 us -> 246 us (level)
  transfers between devices with their start and end apart: 2 -> 2, of which waited for: 2 -> 1; matrix products, arithmetic and copies ran while one was open for 0% -> 0% of each run, Pallas kernels for 3% -> 3%
where the time goes in v7:
time: 246 us; the launch traced here: 245 us
  Pallas kernels  243 us (99%)
    pallas_call x1, Pallas kernels, gather_all(): pl.pallas_call(functools.partial(gather_kernel, shards, widths), out_shap...  234 us
    pallas_call x1, Pallas kernels, write_out(): pl.pallas_call(write_kernel, out_shape=tuple((jax.ShapeDtypeStruct(a.shap...  8.41 us
  transfers between devices with their start and end apart: 2, of which 1 were waited for; matrix products, arithmetic and copies ran while one was open for 0% of the time, Pallas kernels for 3%

profile of v7, /device:TPU:0, one launch (start us, length us, event | category | flops | bytes accessed | tf_op | source)
XLA Modules:
  0.0 245.4 jit_solution(8816520181422206693)
XLA Ops:
  0.6 233.7 %shard_map.138 = (bf16[2048,2048]{1,0:T(8,128)(2,1)S(1)}, bf16[2048,2048]{1,0:T(8,128)(2,1)S(1)}, bf16[2048,2048]{1,0:T(8,128)(2,1)S(1)}, f32[32,1,128]{2,1,0:T(...) custom-call(bf16[256,2048]{1,0:T(8,128)(2,1)} %w_gate.1, bf16[64,256]{1,0:T(8,128)(2,1)} %bitcast.9, ...), custom_call_target="tpu_custom_call" | custom-call | tf_op jit(solution)/shard_map/pallas_call | solution.py:375
  234.3 0.1 collective-permute-start
  234.4 1.6 collective-permute-start.1
  236.0 8.4 %shard_map.139 = (bf16[2048,2048]{1,0:T(8,128)(2,1)}, bf16[2048,2048]{1,0:T(8,128)(2,1)}, bf16[2048,2048]{1,0:T(8,128)(2,1)}, bf16[16,128]{1,0:T(8,128)(2,1)}) custom-call(bf16[2048,2048]{1,0:T(8,128)(2,1)S(1)} %get-tuple-element.16.gate, bf16[2048,2048]{1,0:T(8,128)(2,1)S(1)} %get-tuple-element.17.up, bf16[2048,2048]{1,0:T(8,128)(2,1)S(1)} %get-tuple-element.18.down, ...), custom_call_target="tpu_custom_call" | custom-call | flops 2000000000 | bytes 50331648 | tf_op jit(solution)/shard_map/pallas_call | solution.py:433
  244.4 0.0 collective-permute-done.late_z
  244.4 0.1 collective-permute-done.1.late_x
  244.5 0.9 shard_map.140
Async XLA Ops:
  234.3 10.1 %collective-permute-start = (bf16[768,256]{1,0:T(8,128)(2,1)S(1)}, bf16[768,256]{1,0:T(8,128)(2,1)S(1)}, u32[]{:S(2)}, u32[]{:S(2)}) collective-permute-start(bf16[768,256]{1,0:T(8,128)(2,1)S(1)} %get-tuple-element.23), channel_id=1, source_target_pairs={{0,8},{4,12},{8,0},{12,4},{16,24},{20,28},{24,16},{28,20},{1,9},{5... | collective-permute-start | bytes 1179656 | tf_op jit(solution)/shard_map/ppermute | solution.py:511
  234.4 10.1 %collective-permute-start.1 = (bf16[256,768]{1,0:T(8,128)(2,1)S(1)}, bf16[256,768]{1,0:T(8,128)(2,1)S(1)}, u32[]{:S(2)}, u32[]{:S(2)}) collective-permute-start(bf16[256,768]{1,0:T(8,128)(2,1)S(1)} %get-tuple-element.24), channel_id=1, source_target_pairs={{0,4},{4,0},{8,12},{12,8},{16,20},{20,16},{24,28},{28,24},{1,5},{5... | collective-permute-start | bytes 1179656 | tf_op jit(solution)/shard_map/ppermute | solution.py:512
